TPU v7x, 32 devices: a whole 2x2x4 slice. The times are simulated.
32 devices in a mesh: stage: 4 (over z), data: 8 (over y, x, core).
Axes of the slice: x: 2, y: 2, z: 4, core: 2. Of those that a mesh axis runs over, the one named last changes fastest.
Arguments:
- inputs: bfloat16 [32, 64, 896], P('data')
- targets: bfloat16 [32, 64, 896], P('data')
- w_up: bfloat16 [12, 896, 4864], P('stage')
- w_down: bfloat16 [12, 4864, 896], P('stage')
Outputs:
- output 1: float32 [], replicated
- output 2: float32 [12, 896, 4864], P('stage', 'data')
- output 3: float32 [12, 4864, 896], P('stage', None, 'data')
All inputs are finite; a program needn't handle non-finite values.
Results may differ from a plain program's by a relative error of at most 0.00938019.
Values are sent between devices in bfloat16 or wider.
A program may use at most 1 GiB of HBM per device.

v0:
```python
import jax
import jax.numpy as jnp
from jax import lax
from jax.sharding import PartitionSpec as P

CONTRACT_LAST = (((1,), (1,)), ((), ()))
CONTRACT_FIRST = (((0,), (0,)), ((), ()))


def layer_forward(h_in, w_one, w_two):
    pre_act = jnp.dot(h_in, w_one, preferred_element_type=jnp.float32).astype(jnp.bfloat16)
    act_out = jax.nn.gelu(pre_act.astype(jnp.float32)).astype(jnp.bfloat16)
    branch = jnp.dot(act_out, w_two, preferred_element_type=jnp.float32)
    return (h_in.astype(jnp.float32) + branch).astype(jnp.bfloat16)


def backward_inputs(h_in, grad_out, w_one, w_two):
    pre_act = jnp.dot(h_in, w_one, preferred_element_type=jnp.float32).astype(jnp.bfloat16)
    pre_wide = pre_act.astype(jnp.float32)
    act_out = jax.nn.gelu(pre_wide).astype(jnp.bfloat16)
    grad_act = lax.dot_general(grad_out, w_two, CONTRACT_LAST, preferred_element_type=jnp.float32).astype(jnp.bfloat16)
    grad_pre = jax.jvp(jax.nn.gelu, (pre_wide,), (grad_act.astype(jnp.float32),))[1].astype(jnp.bfloat16)
    back_sum = lax.dot_general(grad_pre, w_one, CONTRACT_LAST, preferred_element_type=jnp.float32)
    grad_in = (grad_out.astype(jnp.float32) + back_sum).astype(jnp.bfloat16)
    return grad_in, act_out, grad_pre


def backward_weights(h_in, act_out, grad_pre, grad_out):
    grad_one = lax.dot_general(h_in, grad_pre, CONTRACT_FIRST, preferred_element_type=jnp.float32)
    grad_two = lax.dot_general(act_out, grad_out, CONTRACT_FIRST, preferred_element_type=jnp.float32)
    return grad_one, grad_two


def solution(mesh):
    stages = mesh.shape['stage']
    replicas = mesh.shape['data']
    fwd_perm = [(src_idx, src_idx + 1) for src_idx in range(stages - 1)]
    bwd_perm = [(src_idx + 1, src_idx) for src_idx in range(stages - 1)]

    def per_device(x_loc, y_loc, w_up, w_down):
        n_micro, n_tokens, n_width = x_loc.shape
        n_layers = w_up.shape[0]
        n_slots = min(n_micro, 2 * stages - 1)
        total_tokens = replicas * n_micro * n_tokens
        stage_idx = lax.axis_index('stage')
        is_first = stage_idx == 0
        is_last = stage_idx == stages - 1
        zero_act = jnp.zeros((n_tokens, n_width), jnp.bfloat16)
        zero_loss = jnp.zeros((), jnp.float32)

        def tick_body(tick_idx, loop_state):
            recv_act, recv_grad, act_store, acc_up, acc_down, loss_acc = loop_state
            fwd_mb = tick_idx - stage_idx
            bwd_mb = tick_idx - (2 * stages - 2) + stage_idx
            fwd_ok = jnp.logical_and(fwd_mb >= 0, fwd_mb < n_micro)
            bwd_ok = jnp.logical_and(bwd_mb >= 0, bwd_mb < n_micro)

            def forward_branch(operands):
                h_prev, stored = operands
                x_mb = lax.dynamic_index_in_dim(x_loc, fwd_mb, 0, keepdims=False)
                hidden = jnp.where(is_first, x_mb, h_prev)
                slot_idx = fwd_mb % n_slots
                for layer_idx in range(n_layers):
                    stored = lax.dynamic_update_slice(stored, hidden[None, None], (slot_idx, layer_idx, 0, 0))
                    hidden = layer_forward(hidden, w_up[layer_idx], w_down[layer_idx])
                y_mb = lax.dynamic_index_in_dim(y_loc, fwd_mb, 0, keepdims=False)
                out_diff = hidden.astype(jnp.float32) - y_mb.astype(jnp.float32)
                part_loss = jnp.where(is_last, jnp.sum(out_diff * out_diff) / (2 * total_tokens), zero_loss)
                top_grad = (out_diff / total_tokens).astype(jnp.bfloat16)
                return hidden, stored, part_loss, top_grad

            def forward_skip(operands):
                h_prev, stored = operands
                return zero_act, stored, zero_loss, zero_act

            send_act, act_store, part_loss, top_grad = lax.cond(fwd_ok, forward_branch, forward_skip, (recv_act, act_store))

            def backward_branch(operands):
                grad_next, stored, up_sums, down_sums = operands
                cur_grad = jnp.where(is_last, top_grad, grad_next)
                saved_block = lax.dynamic_index_in_dim(stored, bwd_mb % n_slots, 0, keepdims=False)
                new_up = list(up_sums)
                new_down = list(down_sums)
                for layer_idx in reversed(range(n_layers)):
                    h_in = saved_block[layer_idx]
                    grad_in, act_out, grad_pre = backward_inputs(h_in, cur_grad, w_up[layer_idx], w_down[layer_idx])
                    grad_one, grad_two = backward_weights(h_in, act_out, grad_pre, cur_grad)
                    new_up[layer_idx] = new_up[layer_idx] + grad_one
                    new_down[layer_idx] = new_down[layer_idx] + grad_two
                    cur_grad = grad_in
                return cur_grad, tuple(new_up), tuple(new_down)

            def backward_skip(operands):
                grad_next, stored, up_sums, down_sums = operands
                return zero_act, up_sums, down_sums

            send_grad, acc_up, acc_down = lax.cond(bwd_ok, backward_branch, backward_skip, (recv_grad, act_store, acc_up, acc_down))
            recv_act = lax.ppermute(send_act, 'stage', fwd_perm)
            recv_grad = lax.ppermute(send_grad, 'stage', bwd_perm)
            return recv_act, recv_grad, act_store, acc_up, acc_down, loss_acc + part_loss

        up_zero = tuple(jnp.zeros(w_up.shape[1:], jnp.float32) for layer_idx in range(n_layers))
        down_zero = tuple(jnp.zeros(w_down.shape[1:], jnp.float32) for layer_idx in range(n_layers))
        store_zero = jnp.zeros((n_slots, n_layers, n_tokens, n_width), jnp.bfloat16)
        init_state = (zero_act, zero_act, store_zero, up_zero, down_zero, zero_loss)
        final_state = lax.fori_loop(0, n_micro + 2 * stages - 2, tick_body, init_state)
        grad_up = lax.psum_scatter(jnp.stack(final_state[3]), 'data', scatter_dimension=1, tiled=True)
        grad_down = lax.psum_scatter(jnp.stack(final_state[4]), 'data', scatter_dimension=2, tiled=True)
        total_loss = lax.psum(final_state[5], ('stage', 'data'))
        return total_loss, grad_up, grad_down

    return jax.shard_map(
        per_device,
        mesh=mesh,
        in_specs=(P('data', None, None), P('data', None, None), P('stage', None, None), P('stage', None, None)),
        out_specs=(P(), P('stage', 'data', None), P('stage', None, 'data')),
        check_vma=False,
    )
```

profile of v0, /device:TPU:0, one launch (start us, length us, event | category | flops | bytes accessed | tf_op | source)
XLA Modules:
  0.0 2012.2 jit_solution(8014156888813677987)
XLA Ops:
  51.7 1285.5 %while.36 = (s32[]{:T(128)}, bf16[64,896]{1,0:T(8,128)(2,1)}, bf16[64,896]{1,0:T(8,128)(2,1)S(1)}, bf16[4,3,64,896]{3,2,1,0:T(8,128)(2,1)}, f32[896,4864]{1,0:T(...) while((s32[]{:T(128)}, bf16[64,896]{1,0:T(8,128)(2,1)}, ...), condition=%wide.region_6.7_spmd, body=%wide.region_0.6_spmd.sunk | while | flops 11783593984 | bytes 497078656 | solution.py:106
  74.1 31.0 %conditional.4 = (bf16[64,896]{1,0:T(8,128)(2,1)}, bf16[4,3,64,896]{3,2,1,0:T(8,128)(2,1)}, f32[]{:T(128)}, bf16[64,896]{1,0:T(8,128)(2,1)S(1)}) conditional(s32[]{:T(128)} %convert_element_type.290, bf16[4,3,64,896]{3,2,1,0:T(8,128)(2,1)} %get-tuple-element.786, (pred[]{:T(512)}, s32[]{:T(128)}, bf16[4,64,896]{2,1,0:T(8,128)(2,1)}, ...), branch_computations={%region_1.0_spmd, %region_2.3_spmd} | conditional | flops 3358416896 | bytes 54365428 | solution.py:76
  75.7 9.4 bitcast_dynamic-update-slice_fusion.1
  94.5 10.0 multiply_convert_fusion
  115.1 31.0 %conditional.4 = (bf16[64,896]{1,0:T(8,128)(2,1)}, bf16[4,3,64,896]{3,2,1,0:T(8,128)(2,1)}, f32[]{:T(128)}, bf16[64,896]{1,0:T(8,128)(2,1)S(1)}) conditional(s32[]{:T(128)} %convert_element_type.290, bf16[4,3,64,896]{3,2,1,0:T(8,128)(2,1)} %get-tuple-element.786, (pred[]{:T(512)}, s32[]{:T(128)}, bf16[4,64,896]{2,1,0:T(8,128)(2,1)}, ...), branch_computations={%region_1.0_spmd, %region_2.3_spmd} | conditional | flops 3358416896 | bytes 54365428 | solution.py:76
  116.7 9.4 bitcast_dynamic-update-slice_fusion.1
  135.5 10.0 multiply_convert_fusion
  155.6 31.0 %conditional.4 = (bf16[64,896]{1,0:T(8,128)(2,1)}, bf16[4,3,64,896]{3,2,1,0:T(8,128)(2,1)}, f32[]{:T(128)}, bf16[64,896]{1,0:T(8,128)(2,1)S(1)}) conditional(s32[]{:T(128)} %convert_element_type.290, bf16[4,3,64,896]{3,2,1,0:T(8,128)(2,1)} %get-tuple-element.786, (pred[]{:T(512)}, s32[]{:T(128)}, bf16[4,64,896]{2,1,0:T(8,128)(2,1)}, ...), branch_computations={%region_1.0_spmd, %region_2.3_spmd} | conditional | flops 3358416896 | bytes 54365428 | solution.py:76
  175.9 10.0 multiply_convert_fusion
  196.1 31.0 %conditional.4 = (bf16[64,896]{1,0:T(8,128)(2,1)}, bf16[4,3,64,896]{3,2,1,0:T(8,128)(2,1)}, f32[]{:T(128)}, bf16[64,896]{1,0:T(8,128)(2,1)S(1)}) conditional(s32[]{:T(128)} %convert_element_type.290, bf16[4,3,64,896]{3,2,1,0:T(8,128)(2,1)} %get-tuple-element.786, (pred[]{:T(512)}, s32[]{:T(128)}, bf16[4,64,896]{2,1,0:T(8,128)(2,1)}, ...), branch_computations={%region_1.0_spmd, %region_2.3_spmd} | conditional | flops 3358416896 | bytes 54365428 | solution.py:76
  216.5 10.0 multiply_convert_fusion
  237.3 32.5 %collective-permute-start = (bf16[64,896]{1,0:T(8,128)(2,1)}, bf16[64,896]{1,0:T(8,128)(2,1)}, u32[]{:S(2)}, u32[]{:S(2)}) collective-permute-start(bf16[64,896]{1,0:T(8,128)(2,1)} %get-tuple-element.728), channel_id=1, source_target_pairs={{0,8},{8,16},{16,24},{1,9},{9,17},{17,25},{2,10},{10,18},{18,26},{... | collective-permute-start | bytes 344072 | tf_op jit(solution)/shard_map/while/body/eval_jaxpr/ppermute | solution.py:98
  271.8 134.0 %collective-permute-done.1 = bf16[64,896]{1,0:T(8,128)(2,1)S(1)} collective-permute-done((bf16[64,896]{1,0:T(8,128)(2,1)}, bf16[64,896]{1,0:T(8,128)(2,1)S(1)}, u32[]{:S(2)}, u32[]{:S(2)}) %collective-permute-start.1) | collective-permute-done | bytes 114720 | tf_op jit(solution)/shard_map/while/body/eval_jaxpr/ppermute | solution.py:99
  406.5 138.4 %collective-permute-start = (bf16[64,896]{1,0:T(8,128)(2,1)}, bf16[64,896]{1,0:T(8,128)(2,1)}, u32[]{:S(2)}, u32[]{:S(2)}) collective-permute-start(bf16[64,896]{1,0:T(8,128)(2,1)} %get-tuple-element.728), channel_id=1, source_target_pairs={{0,8},{8,16},{16,24},{1,9},{9,17},{17,25},{2,10},{10,18},{18,26},{... | collective-permute-start | bytes 344072 | tf_op jit(solution)/shard_map/while/body/eval_jaxpr/ppermute | solution.py:98
  546.8 171.0 %collective-permute-done.1 = bf16[64,896]{1,0:T(8,128)(2,1)S(1)} collective-permute-done((bf16[64,896]{1,0:T(8,128)(2,1)}, bf16[64,896]{1,0:T(8,128)(2,1)S(1)}, u32[]{:S(2)}, u32[]{:S(2)}) %collective-permute-start.1) | collective-permute-done | bytes 114720 | tf_op jit(solution)/shard_map/while/body/eval_jaxpr/ppermute | solution.py:99
  723.1 136.5 %conditional.5 = (bf16[64,896]{1,0:T(8,128)(2,1)}, f32[896,4864]{1,0:T(8,128)}, f32[896,4864]{1,0:T(8,128)}, f32[896,4864]{1,0:T(8,128)}, f32[4864,896]{1,0:T(8,...) conditional(s32[]{:T(128)} %convert_element_type.291, (f32[896,4864]{1,0:T(8,128)}, f32[896,4864]{1,0:T(8,128)}, ...), branch_computations={%region_4.4_spmd, %region_5.5_spmd} | conditional | flops 8425177088 | bytes 441795168 | solution.py:97
  776.7 13.5 convolution_add_fusion.2
  790.2 15.7 convolution_add_fusion.1
  809.7 20.9 %convolution_add_fusion.4 = f32[896,4864]{1,0:T(8,128)} fusion(f32[896,4864]{1,0:T(8,128)} %get-tuple-element.513, bf16[64,4864]{1,0:T(8,128)(2,1)} %copy-done.4, bf16[4,3,64,896]{3,2,1,0:T(8,128)(2,1)} %get-tuple-element.509, s32[]{:T(128)S(6)} %select_n.42, s32[]{:T(128)S(6)} %add.164), kind=kOutput, calls=%fused_computation.93 | convolution fusion | flops 562200576 | bytes 35602440 | tf_op jit(solution)/shard_map/while/body/eval_jaxpr/cond/branch_1_fun/dot_general | solution.py:29
  830.6 14.5 convolution_add_fusion.3
  845.1 14.4 convolution_add_fusion.5
  866.9 30.0 %collective-permute-start = (bf16[64,896]{1,0:T(8,128)(2,1)}, bf16[64,896]{1,0:T(8,128)(2,1)}, u32[]{:S(2)}, u32[]{:S(2)}) collective-permute-start(bf16[64,896]{1,0:T(8,128)(2,1)} %get-tuple-element.728), channel_id=1, source_target_pairs={{0,8},{8,16},{16,24},{1,9},{9,17},{17,25},{2,10},{10,18},{18,26},{... | collective-permute-start | bytes 344072 | tf_op jit(solution)/shard_map/while/body/eval_jaxpr/ppermute | solution.py:98
  896.8 136.5 %conditional.5 = (bf16[64,896]{1,0:T(8,128)(2,1)}, f32[896,4864]{1,0:T(8,128)}, f32[896,4864]{1,0:T(8,128)}, f32[896,4864]{1,0:T(8,128)}, f32[4864,896]{1,0:T(8,...) conditional(s32[]{:T(128)} %convert_element_type.291, (f32[896,4864]{1,0:T(8,128)}, f32[896,4864]{1,0:T(8,128)}, ...), branch_computations={%region_4.4_spmd, %region_5.5_spmd} | conditional | flops 8425177088 | bytes 441795168 | solution.py:97
  950.5 13.5 convolution_add_fusion.2
  964.0 15.7 convolution_add_fusion.1
  983.5 20.9 %convolution_add_fusion.4 = f32[896,4864]{1,0:T(8,128)} fusion(f32[896,4864]{1,0:T(8,128)} %get-tuple-element.513, bf16[64,4864]{1,0:T(8,128)(2,1)} %copy-done.4, bf16[4,3,64,896]{3,2,1,0:T(8,128)(2,1)} %get-tuple-element.509, s32[]{:T(128)S(6)} %select_n.42, s32[]{:T(128)S(6)} %add.164), kind=kOutput, calls=%fused_computation.93 | convolution fusion | flops 562200576 | bytes 35602440 | tf_op jit(solution)/shard_map/while/body/eval_jaxpr/cond/branch_1_fun/dot_general | solution.py:29
  1004.4 14.5 convolution_add_fusion.3
  1018.9 14.4 convolution_add_fusion.5
  1044.6 136.5 %conditional.5 = (bf16[64,896]{1,0:T(8,128)(2,1)}, f32[896,4864]{1,0:T(8,128)}, f32[896,4864]{1,0:T(8,128)}, f32[896,4864]{1,0:T(8,128)}, f32[4864,896]{1,0:T(8,...) conditional(s32[]{:T(128)} %convert_element_type.291, (f32[896,4864]{1,0:T(8,128)}, f32[896,4864]{1,0:T(8,128)}, ...), branch_computations={%region_4.4_spmd, %region_5.5_spmd} | conditional | flops 8425177088 | bytes 441795168 | solution.py:97
  1098.3 13.5 convolution_add_fusion.2
  1111.8 15.7 convolution_add_fusion.1
  1131.3 20.9 %convolution_add_fusion.4 = f32[896,4864]{1,0:T(8,128)} fusion(f32[896,4864]{1,0:T(8,128)} %get-tuple-element.513, bf16[64,4864]{1,0:T(8,128)(2,1)} %copy-done.4, bf16[4,3,64,896]{3,2,1,0:T(8,128)(2,1)} %get-tuple-element.509, s32[]{:T(128)S(6)} %select_n.42, s32[]{:T(128)S(6)} %add.164), kind=kOutput, calls=%fused_computation.93 | convolution fusion | flops 562200576 | bytes 35602440 | tf_op jit(solution)/shard_map/while/body/eval_jaxpr/cond/branch_1_fun/dot_general | solution.py:29
  1152.2 14.5 convolution_add_fusion.3
  1166.7 14.4 convolution_add_fusion.5
  1191.5 136.5 %conditional.5 = (bf16[64,896]{1,0:T(8,128)(2,1)}, f32[896,4864]{1,0:T(8,128)}, f32[896,4864]{1,0:T(8,128)}, f32[896,4864]{1,0:T(8,128)}, f32[4864,896]{1,0:T(8,...) conditional(s32[]{:T(128)} %convert_element_type.291, (f32[896,4864]{1,0:T(8,128)}, f32[896,4864]{1,0:T(8,128)}, ...), branch_computations={%region_4.4_spmd, %region_5.5_spmd} | conditional | flops 8425177088 | bytes 441795168 | solution.py:97
  1245.1 13.5 convolution_add_fusion.2
  1258.6 15.7 convolution_add_fusion.1
  1278.1 20.9 %convolution_add_fusion.4 = f32[896,4864]{1,0:T(8,128)} fusion(f32[896,4864]{1,0:T(8,128)} %get-tuple-element.513, bf16[64,4864]{1,0:T(8,128)(2,1)} %copy-done.4, bf16[4,3,64,896]{3,2,1,0:T(8,128)(2,1)} %get-tuple-element.509, s32[]{:T(128)S(6)} %select_n.42, s32[]{:T(128)S(6)} %add.164), kind=kOutput, calls=%fused_computation.93 | convolution fusion | flops 562200576 | bytes 35602440 | tf_op jit(solution)/shard_map/while/body/eval_jaxpr/cond/branch_1_fun/dot_general | solution.py:29
  1299.0 14.5 convolution_add_fusion.3
  1313.5 14.4 convolution_add_fusion.5
  1337.2 19.0 copy.7
  1356.1 18.9 copy.8
  1375.0 18.9 copy.9
  1393.9 35.0 %pad_maximum_fusion.1 = f32[3,4864,896]{1,2,0:T(8,128)} fusion(f32[1,4864,896]{1,2,0:T(8,128)} %bitcast.198, f32[1,4864,896]{1,2,0:T(8,128)} %bitcast.197, f32[1,4864,896]{1,2,0:T(8,128)} %bitcast.196), kind=kLoop, calls=%fused_computation.223 | loop fusion | flops 26148864 | bytes 104595456 | tf_op jit(solution)/shard_map/stack | solution.py:108
  1429.0 35.0 %pad_maximum_fusion = f32[3,896,4864]{2,1,0:T(8,128)} fusion(f32[1,896,4864]{2,1,0:T(8,128)} %bitcast.194, f32[1,896,4864]{2,1,0:T(8,128)} %bitcast.195, f32[1,896,4864]{2,1,0:T(8,128)} %bitcast.193), kind=kLoop, calls=%fused_computation.222 | loop fusion | flops 26148864 | bytes 104595456 | tf_op jit(solution)/shard_map/stack | solution.py:107
  1464.0 39.8 %psum.7 = f32[]{:T(128)} all-reduce(f32[]{:T(128)} %get-tuple-element.558), channel_id=1, replica_groups=mesh['stage'=4,'data'=8] {'stage','data'}, use_global_device_ids=true, to_apply=%region_7.8 | all-reduce | flops 1 | bytes 8 | tf_op jit(solution)/shard_map/psum | solution.py:109
  1503.8 210.8 %reduce-scatter.5.cloned.1.call-done = f32[3,4864,112]{1,2,0:T(8,128)} async-done(((f32[3,4864,896]{1,2,0:T(8,128)}), f32[3,4864,112]{1,2,0:T(8,128)}) %reduce-scatter.5.cloned.1.call-update) | async-done | bytes 6537232 | tf_op jit(solution)/shard_map/reduce_scatter | solution.py:108
  1714.6 290.5 %reduce-scatter.3.cloned.1.call-done = f32[3,112,4864]{2,1,0:T(8,128)} async-done(((f32[3,896,4864]{2,1,0:T(8,128)}), f32[3,112,4864]{2,1,0:T(8,128)}) %reduce-scatter.3.cloned.1.call-update) | async-done | bytes 6537232 | tf_op jit(solution)/shard_map/reduce_scatter | solution.py:107
  (224 shorter events, 428.5 us)
Async XLA Ops:
  7.2 1707.5 %reduce-scatter.5.cloned.1.call-start = ((), (), s32[]{:S(2)}) async-start(), calls=%async_computation.3 | async-start | bytes 58834944 | tf_op jit(solution)/shard_map/reduce_scatter | solution.py:108
  105.1 4.6 collective-permute-start
  107.7 7.4 collective-permute-start.1
  146.1 4.1 collective-permute-start
  148.9 6.7 collective-permute-start.1
  186.6 4.2 collective-permute-start
  189.5 6.7 collective-permute-start.1
  227.1 4.2 collective-permute-start
  230.0 6.7 collective-permute-start.1
  237.3 34.5 %collective-permute-start = (bf16[64,896]{1,0:T(8,128)(2,1)}, bf16[64,896]{1,0:T(8,128)(2,1)}, u32[]{:S(2)}, u32[]{:S(2)}) collective-permute-start(bf16[64,896]{1,0:T(8,128)(2,1)} %get-tuple-element.728), channel_id=1, source_target_pairs={{0,8},{8,16},{16,24},{1,9},{9,17},{17,25},{2,10},{10,18},{18,26},{... | collective-permute-start | bytes 344072 | tf_op jit(solution)/shard_map/while/body/eval_jaxpr/ppermute | solution.py:98
  270.5 135.3 %collective-permute-start.1 = (bf16[64,896]{1,0:T(8,128)(2,1)}, bf16[64,896]{1,0:T(8,128)(2,1)S(1)}, u32[]{:S(2)}, u32[]{:S(2)}) collective-permute-start(bf16[64,896]{1,0:T(8,128)(2,1)} %get-tuple-element.731), channel_id=1, source_target_pairs={{8,0},{16,8},{24,16},{9,1},{17,9},{25,17},{10,2},{18,10},{26,18},{... | collective-permute-start | bytes 344072 | tf_op jit(solution)/shard_map/while/body/eval_jaxpr/ppermute | solution.py:99
  406.5 140.3 %collective-permute-start = (bf16[64,896]{1,0:T(8,128)(2,1)}, bf16[64,896]{1,0:T(8,128)(2,1)}, u32[]{:S(2)}, u32[]{:S(2)}) collective-permute-start(bf16[64,896]{1,0:T(8,128)(2,1)} %get-tuple-element.728), channel_id=1, source_target_pairs={{0,8},{8,16},{16,24},{1,9},{9,17},{17,25},{2,10},{10,18},{18,26},{... | collective-permute-start | bytes 344072 | tf_op jit(solution)/shard_map/while/body/eval_jaxpr/ppermute | solution.py:98
  545.5 172.3 %collective-permute-start.1 = (bf16[64,896]{1,0:T(8,128)(2,1)}, bf16[64,896]{1,0:T(8,128)(2,1)S(1)}, u32[]{:S(2)}, u32[]{:S(2)}) collective-permute-start(bf16[64,896]{1,0:T(8,128)(2,1)} %get-tuple-element.731), channel_id=1, source_target_pairs={{8,0},{16,8},{24,16},{9,1},{17,9},{25,17},{10,2},{18,10},{26,18},{... | collective-permute-start | bytes 344072 | tf_op jit(solution)/shard_map/while/body/eval_jaxpr/ppermute | solution.py:99
  718.5 142.3 %collective-permute-start = (bf16[64,896]{1,0:T(8,128)(2,1)}, bf16[64,896]{1,0:T(8,128)(2,1)}, u32[]{:S(2)}, u32[]{:S(2)}) collective-permute-start(bf16[64,896]{1,0:T(8,128)(2,1)} %get-tuple-element.728), channel_id=1, source_target_pairs={{0,8},{8,16},{16,24},{1,9},{9,17},{17,25},{2,10},{10,18},{18,26},{... | collective-permute-start | bytes 344072 | tf_op jit(solution)/shard_map/while/body/eval_jaxpr/ppermute | solution.py:98
  727.9 18.0 copy-start.1
  776.7 29.3 %slice-start = ((s8[17432576]{0:T(1024)(128)(4,1)}), s8[4194304]{0:T(1024)(128)(4,1)S(1)}, s32[]{:S(2)}) async-start(s8[17432576]{0:T(1024)(128)(4,1)} %bitcast.191), calls=%async_computation.4 | async-start | bytes 8388608 | tf_op jit(solution)/shard_map/while/body/eval_jaxpr/cond
  776.7 29.3 %slice-start.1 = ((s8[17432576]{0:T(1024)(128)(4,1)}), s8[4194304]{0:T(1024)(128)(4,1)S(1)}, s32[]{:S(2)}) async-start(s8[17432576]{0:T(1024)(128)(4,1)} %bitcast.191), calls=%async_computation.5 | async-start | bytes 8388608 | tf_op jit(solution)/shard_map/while/body/eval_jaxpr/cond
  776.7 29.3 %slice-start.2 = ((s8[17432576]{0:T(1024)(128)(4,1)}), s8[4194304]{0:T(1024)(128)(4,1)S(1)}, s32[]{:S(2)}) async-start(s8[17432576]{0:T(1024)(128)(4,1)} %bitcast.191), calls=%async_computation.6 | async-start | bytes 8388608 | tf_op jit(solution)/shard_map/while/body/eval_jaxpr/cond
  809.7 20.9 %copy-start = (f32[4864,896]{1,0:T(8,128)}, f32[4864,896]{1,0:T(8,128)S(1)}, u32[]{:S(2)}) copy-start(f32[4864,896]{1,0:T(8,128)S(1)} %convolution_add_fusion) | copy-start | bytes 52297732 | tf_op jit(solution)/shard_map/while/body/eval_jaxpr/cond
  809.7 20.9 %copy-start.3 = (bf16[64,4864]{1,0:T(8,128)(2,1)S(1)}, bf16[64,4864]{1,0:T(8,128)(2,1)}, u32[]{:S(2)}) copy-start(bf16[64,4864]{1,0:T(8,128)(2,1)} %copy-done.2) | copy-start | bytes 1867780 | tf_op jit(solution)/shard_map/while/body/eval_jaxpr/cond
  859.5 6.7 collective-permute-start.1
  866.9 167.7 %collective-permute-start = (bf16[64,896]{1,0:T(8,128)(2,1)}, bf16[64,896]{1,0:T(8,128)(2,1)}, u32[]{:S(2)}, u32[]{:S(2)}) collective-permute-start(bf16[64,896]{1,0:T(8,128)(2,1)} %get-tuple-element.728), channel_id=1, source_target_pairs={{0,8},{8,16},{16,24},{1,9},{9,17},{17,25},{2,10},{10,18},{18,26},{... | collective-permute-start | bytes 344072 | tf_op jit(solution)/shard_map/while/body/eval_jaxpr/ppermute | solution.py:98
  901.7 18.0 copy-start.1
  950.4 29.3 %slice-start = ((s8[17432576]{0:T(1024)(128)(4,1)}), s8[4194304]{0:T(1024)(128)(4,1)S(1)}, s32[]{:S(2)}) async-start(s8[17432576]{0:T(1024)(128)(4,1)} %bitcast.191), calls=%async_computation.4 | async-start | bytes 8388608 | tf_op jit(solution)/shard_map/while/body/eval_jaxpr/cond
  950.5 29.3 %slice-start.1 = ((s8[17432576]{0:T(1024)(128)(4,1)}), s8[4194304]{0:T(1024)(128)(4,1)S(1)}, s32[]{:S(2)}) async-start(s8[17432576]{0:T(1024)(128)(4,1)} %bitcast.191), calls=%async_computation.5 | async-start | bytes 8388608 | tf_op jit(solution)/shard_map/while/body/eval_jaxpr/cond
  950.5 29.3 %slice-start.2 = ((s8[17432576]{0:T(1024)(128)(4,1)}), s8[4194304]{0:T(1024)(128)(4,1)S(1)}, s32[]{:S(2)}) async-start(s8[17432576]{0:T(1024)(128)(4,1)} %bitcast.191), calls=%async_computation.6 | async-start | bytes 8388608 | tf_op jit(solution)/shard_map/while/body/eval_jaxpr/cond
  964.0 15.8 slice-start.4
  983.5 20.9 %copy-start = (f32[4864,896]{1,0:T(8,128)}, f32[4864,896]{1,0:T(8,128)S(1)}, u32[]{:S(2)}) copy-start(f32[4864,896]{1,0:T(8,128)S(1)} %convolution_add_fusion) | copy-start | bytes 52297732 | tf_op jit(solution)/shard_map/while/body/eval_jaxpr/cond
  983.5 20.9 %copy-start.3 = (bf16[64,4864]{1,0:T(8,128)(2,1)S(1)}, bf16[64,4864]{1,0:T(8,128)(2,1)}, u32[]{:S(2)}) copy-start(bf16[64,4864]{1,0:T(8,128)(2,1)} %copy-done.2) | copy-start | bytes 1867780 | tf_op jit(solution)/shard_map/while/body/eval_jaxpr/cond
  1033.3 6.7 collective-permute-start.1
  1040.7 141.8 %collective-permute-start = (bf16[64,896]{1,0:T(8,128)(2,1)}, bf16[64,896]{1,0:T(8,128)(2,1)}, u32[]{:S(2)}, u32[]{:S(2)}) collective-permute-start(bf16[64,896]{1,0:T(8,128)(2,1)} %get-tuple-element.728), channel_id=1, source_target_pairs={{0,8},{8,16},{16,24},{1,9},{9,17},{17,25},{2,10},{10,18},{18,26},{... | collective-permute-start | bytes 344072 | tf_op jit(solution)/shard_map/while/body/eval_jaxpr/ppermute | solution.py:98
  1049.5 18.0 copy-start.1
  1098.3 29.3 %slice-start = ((s8[17432576]{0:T(1024)(128)(4,1)}), s8[4194304]{0:T(1024)(128)(4,1)S(1)}, s32[]{:S(2)}) async-start(s8[17432576]{0:T(1024)(128)(4,1)} %bitcast.191), calls=%async_computation.4 | async-start | bytes 8388608 | tf_op jit(solution)/shard_map/while/body/eval_jaxpr/cond
  1098.3 29.3 %slice-start.1 = ((s8[17432576]{0:T(1024)(128)(4,1)}), s8[4194304]{0:T(1024)(128)(4,1)S(1)}, s32[]{:S(2)}) async-start(s8[17432576]{0:T(1024)(128)(4,1)} %bitcast.191), calls=%async_computation.5 | async-start | bytes 8388608 | tf_op jit(solution)/shard_map/while/body/eval_jaxpr/cond
  1098.3 29.3 %slice-start.2 = ((s8[17432576]{0:T(1024)(128)(4,1)}), s8[4194304]{0:T(1024)(128)(4,1)S(1)}, s32[]{:S(2)}) async-start(s8[17432576]{0:T(1024)(128)(4,1)} %bitcast.191), calls=%async_computation.6 | async-start | bytes 8388608 | tf_op jit(solution)/shard_map/while/body/eval_jaxpr/cond
  1111.8 15.8 slice-start.4
  1131.3 20.9 %copy-start = (f32[4864,896]{1,0:T(8,128)}, f32[4864,896]{1,0:T(8,128)S(1)}, u32[]{:S(2)}) copy-start(f32[4864,896]{1,0:T(8,128)S(1)} %convolution_add_fusion) | copy-start | bytes 52297732 | tf_op jit(solution)/shard_map/while/body/eval_jaxpr/cond
  1131.3 20.9 %copy-start.3 = (bf16[64,4864]{1,0:T(8,128)(2,1)S(1)}, bf16[64,4864]{1,0:T(8,128)(2,1)}, u32[]{:S(2)}) copy-start(bf16[64,4864]{1,0:T(8,128)(2,1)} %copy-done.2) | copy-start | bytes 1867780 | tf_op jit(solution)/shard_map/while/body/eval_jaxpr/cond
  1181.1 6.7 collective-permute-start.1
  1188.5 140.8 %collective-permute-start = (bf16[64,896]{1,0:T(8,128)(2,1)}, bf16[64,896]{1,0:T(8,128)(2,1)}, u32[]{:S(2)}, u32[]{:S(2)}) collective-permute-start(bf16[64,896]{1,0:T(8,128)(2,1)} %get-tuple-element.728), channel_id=1, source_target_pairs={{0,8},{8,16},{16,24},{1,9},{9,17},{17,25},{2,10},{10,18},{18,26},{... | collective-permute-start | bytes 344072 | tf_op jit(solution)/shard_map/while/body/eval_jaxpr/ppermute | solution.py:98
  1196.3 18.0 copy-start.1
  1245.1 29.3 %slice-start = ((s8[17432576]{0:T(1024)(128)(4,1)}), s8[4194304]{0:T(1024)(128)(4,1)S(1)}, s32[]{:S(2)}) async-start(s8[17432576]{0:T(1024)(128)(4,1)} %bitcast.191), calls=%async_computation.4 | async-start | bytes 8388608 | tf_op jit(solution)/shard_map/while/body/eval_jaxpr/cond
  1245.1 29.3 %slice-start.1 = ((s8[17432576]{0:T(1024)(128)(4,1)}), s8[4194304]{0:T(1024)(128)(4,1)S(1)}, s32[]{:S(2)}) async-start(s8[17432576]{0:T(1024)(128)(4,1)} %bitcast.191), calls=%async_computation.5 | async-start | bytes 8388608 | tf_op jit(solution)/shard_map/while/body/eval_jaxpr/cond
  1245.1 29.3 %slice-start.2 = ((s8[17432576]{0:T(1024)(128)(4,1)}), s8[4194304]{0:T(1024)(128)(4,1)S(1)}, s32[]{:S(2)}) async-start(s8[17432576]{0:T(1024)(128)(4,1)} %bitcast.191), calls=%async_computation.6 | async-start | bytes 8388608 | tf_op jit(solution)/shard_map/while/body/eval_jaxpr/cond
  1278.1 20.9 %copy-start = (f32[4864,896]{1,0:T(8,128)}, f32[4864,896]{1,0:T(8,128)S(1)}, u32[]{:S(2)}) copy-start(f32[4864,896]{1,0:T(8,128)S(1)} %convolution_add_fusion) | copy-start | bytes 52297732 | tf_op jit(solution)/shard_map/while/body/eval_jaxpr/cond
  1278.1 20.9 %copy-start.3 = (bf16[64,4864]{1,0:T(8,128)(2,1)S(1)}, bf16[64,4864]{1,0:T(8,128)(2,1)}, u32[]{:S(2)}) copy-start(bf16[64,4864]{1,0:T(8,128)(2,1)} %copy-done.2) | copy-start | bytes 1867780 | tf_op jit(solution)/shard_map/while/body/eval_jaxpr/cond
  1327.9 6.7 collective-permute-start.1
  1428.9 576.2 %reduce-scatter.3.cloned.1.call-start = ((), (), s32[]{:S(2)}) async-start(), calls=%async_computation.2 | async-start | bytes 58834944 | tf_op jit(solution)/shard_map/reduce_scatter | solution.py:107
  (18 other events, 171.4 us)
Sparse Core Ops, SparseCore 0:
  1429.1 285.5 reduce-scatter.4
  1718.9 286.1 reduce-scatter.2
where the time goes:
time: 2020 us; the launch traced here: 2010 us
  waiting for transfers between devices  850 us (42%)
  matrix products  660 us (33%)
  starting transfers between devices  234 us (12%)
  local copies, waits for them, and re-layouts  109 us (5%)
  other arithmetic  76.3 us (4%)
  blocking collectives  39.8 us (2%)
  loops' own time  28.6 us (1%)
    ppermute x10, waiting for transfers between devices, tick_body(): recv_grad = lax.ppermute(send_grad, 'stage', bwd_perm)  348 us
    reduce_scatter x1, waiting for transfers between devices, per_device(): lax.psum_scatter(jnp.stack(final_state[3]), 'data', scatter_dimension=1,...  290 us
    ppermute x10, starting transfers between devices, tick_body(): recv_act = lax.ppermute(send_act, 'stage', fwd_perm)  221 us
    reduce_scatter x1, waiting for transfers between devices, per_device(): lax.psum_scatter(jnp.stack(final_state[4]), 'data', scatter_dimension=2,...  211 us
    dot_general x12, matrix products, backward_weights(): lax.dot_general(h_in, grad_pre, CONTRACT_FIRST, preferred_element_type=jn...  199 us
    dot_general x12, matrix products, backward_weights(): lax.dot_general(act_out, grad_out, CONTRACT_FIRST, preferred_element_type...  132 us
    dot_general x12, matrix products, layer_forward(): branch = jnp.dot(act_out, w_two, preferred_element_type=jnp.float32)  115 us
    dot_general x12, matrix products, backward_inputs(): lax.dot_general(grad_pre, w_one, CONTRACT_LAST, preferred_element_type=jn...  79.2 us
  transfers between devices with their start and end apart: 22, of which 13 were waited for; matrix products, arithmetic and copies ran while one was open for 29% of the time, Pallas kernels for 0%

commit v1 on v0

v1 whole, which is shorter than its diff:
```python
import jax
import jax.numpy as jnp
from jax import lax
from jax.sharding import PartitionSpec as P

CONTRACT_LAST = (((1,), (1,)), ((), ()))
CONTRACT_FIRST = (((0,), (0,)), ((), ()))
SAME_CORE = [[0, 2, 4, 6], [1, 3, 5, 7]]
SWAP_CORE = [(0, 1), (1, 0), (2, 3), (3, 2), (4, 5), (5, 4), (6, 7), (7, 6)]


def up_proj(h_in, w_one):
    return jnp.dot(h_in, w_one, preferred_element_type=jnp.float32).astype(jnp.bfloat16)


def gelu_of(pre_act):
    return jax.nn.gelu(pre_act.astype(jnp.float32)).astype(jnp.bfloat16)


def grad_pre_of(grad_out, pre_act, w_two):
    grad_act = lax.dot_general(grad_out, w_two, CONTRACT_LAST, preferred_element_type=jnp.float32).astype(jnp.bfloat16)
    return jax.jvp(jax.nn.gelu, (pre_act.astype(jnp.float32),), (grad_act.astype(jnp.float32),))[1].astype(jnp.bfloat16)


def solution(mesh):
    stages = mesh.shape['stage']
    replicas = mesh.shape['data']
    fwd_perm = [(s, s + 1) for s in range(stages - 1)]
    bwd_perm = [(s + 1, s) for s in range(stages - 1)]

    def per_device(x_loc, y_loc, w_up, w_down):
        n_micro, n_tokens, n_width = x_loc.shape
        n_layers = w_up.shape[0]
        rows = n_micro * n_tokens
        total_tokens = replicas * rows
        stage_idx = lax.axis_index('stage')
        data_idx = lax.axis_index('data')
        x_rows = x_loc.reshape(rows, n_width)
        y_rows = y_loc.reshape(rows, n_width)
        zero_act = jnp.zeros((rows, n_width), jnp.bfloat16)

        hidden = x_rows
        h_saved = tuple(zero_act for _ in range(n_layers))
        u_saved = tuple(jnp.zeros((rows, w_up.shape[2]), jnp.bfloat16) for _ in range(n_layers))
        for tick in range(stages):
            def run_fwd(operands):
                h_cur, _, _ = operands
                hs, us = [], []
                for layer in range(n_layers):
                    hs.append(h_cur)
                    u = up_proj(h_cur, w_up[layer])
                    us.append(u)
                    branch = jnp.dot(gelu_of(u), w_down[layer], preferred_element_type=jnp.float32)
                    h_cur = (h_cur.astype(jnp.float32) + branch).astype(jnp.bfloat16)
                return h_cur, tuple(hs), tuple(us)

            hidden, h_saved, u_saved = lax.cond(stage_idx == tick, run_fwd, lambda ops: ops, (hidden, h_saved, u_saved))
            if tick < stages - 1:
                recv = lax.ppermute(hidden, 'stage', fwd_perm)
                hidden = jnp.where(stage_idx == tick + 1, recv, hidden)

        is_last = stage_idx == stages - 1
        out_diff = hidden.astype(jnp.float32) - y_rows.astype(jnp.float32)
        part_loss = jnp.where(is_last, jnp.sum(out_diff * out_diff) / (2 * total_tokens), 0.0)
        total_loss = lax.psum(part_loss, ('stage', 'data'))
        grad = (out_diff / total_tokens).astype(jnp.bfloat16)

        h_all = [lax.all_gather(h, 'data', axis_index_groups=SAME_CORE, tiled=True) for h in h_saved]

        e_saved = tuple(zero_act for _ in range(n_layers))
        for tick in reversed(range(stages)):
            def run_bwd(operands):
                e_cur, _ = operands
                es = [None] * n_layers
                for layer in reversed(range(n_layers)):
                    es[layer] = e_cur
                    du = grad_pre_of(e_cur, u_saved[layer], w_down[layer])
                    back = lax.dot_general(du, w_up[layer], CONTRACT_LAST, preferred_element_type=jnp.float32)
                    e_cur = (e_cur.astype(jnp.float32) + back).astype(jnp.bfloat16)
                return e_cur, tuple(es)

            grad, e_saved = lax.cond(stage_idx == tick, run_bwd, lambda ops: ops, (grad, e_saved))
            if tick > 0:
                recv = lax.ppermute(grad, 'stage', bwd_perm)
                grad = jnp.where(stage_idx == tick - 1, recv, grad)

        e_all = [lax.all_gather(e, 'data', axis_index_groups=SAME_CORE, tiled=True) for e in e_saved]

        chip = data_idx // 2
        core = data_idx % 2
        width_blk = n_width // replicas
        up_out, down_out = [], []
        for layer in range(n_layers):
            u = up_proj(h_all[layer], w_up[layer])
            g = gelu_of(u)
            du = grad_pre_of(e_all[layer], u, w_down[layer])
            h_cols = lax.dynamic_slice_in_dim(h_all[layer], chip * 2 * width_blk, 2 * width_blk, 1)
            e_cols = lax.dynamic_slice_in_dim(e_all[layer], chip * 2 * width_blk, 2 * width_blk, 1)
            g_one = lax.dot_general(h_cols, du, CONTRACT_FIRST, preferred_element_type=jnp.float32)
            g_two = lax.dot_general(g, e_cols, CONTRACT_FIRST, preferred_element_type=jnp.float32)
            send_one = lax.dynamic_slice_in_dim(g_one, (1 - core) * width_blk, width_blk, 0)
            keep_one = lax.dynamic_slice_in_dim(g_one, core * width_blk, width_blk, 0)
            send_two = lax.dynamic_slice_in_dim(g_two, (1 - core) * width_blk, width_blk, 1)
            keep_two = lax.dynamic_slice_in_dim(g_two, core * width_blk, width_blk, 1)
            up_out.append(keep_one + lax.ppermute(send_one, 'data', SWAP_CORE))
            down_out.append(keep_two + lax.ppermute(send_two, 'data', SWAP_CORE))
        return total_loss, jnp.stack(up_out), jnp.stack(down_out)

    return jax.shard_map(
        per_device,
        mesh=mesh,
        in_specs=(P('data', None, None), P('data', None, None), P('stage', None, None), P('stage', None, None)),
        out_specs=(P(), P('stage', 'data', None), P('stage', None, 'data')),
        check_vma=False,
    )
```

time: 2020 us -> 661 us (0.33)
  waiting for transfers between devices: 850 us -> 243 us
  matrix products: 660 us -> 230 us
  starting transfers between devices: 234 us -> 55.5 us
  local copies, waits for them, and re-layouts: 109 us -> 17.7 us
  other arithmetic: 76.3 us -> 20.9 us
    reduce_scatter x2 -> x0, waiting for transfers between devices: 501 us -> none  [the longest x1 290 us: per_device(): lax.psum_scatter(jnp.stack(final_state[3]), 'data', scatter_dimension=1,...]
    dot_general x72 -> x17, matrix products: 660 us -> 230 us  [the longest x3 78.3 us: per_device(): lax.dot_general(h_cols, du, CONTRACT_FIRST, preferred_element_type=jnp.fl...]
    ppermute x20 -> x12, starting transfers between devices: 234 us -> 55.3 us  [the longest x3 49.8 us: per_device(): recv = lax.ppermute(hidden, 'stage', fwd_perm)]
    ppermute x20 -> x12, waiting for transfers between devices: 349 us -> 241 us  [the longest x3 212 us: per_device(): recv = lax.ppermute(grad, 'stage', bwd_perm)]
    while x3 -> x0, local copies, waits for them, and re-layouts: 56.8 us -> none  [per_device(): lax.fori_loop(0, n_micro + 2 * stages - 2, tick_body, init_state)]
    another operation x2 -> x8, other arithmetic: 70 us -> 17.7 us  [per_device(): return (total_loss, jnp.stack(up_out), jnp.stack(down_out))]
    another operation x6 -> x0, local copies, waits for them, and re-layouts: 42.5 us -> none
  transfers between devices with their start and end apart: 22 -> 18, of which waited for: 13 -> 6; matrix products, arithmetic and copies ran while one was open for 29% -> 33% of each run, Pallas kernels for 0% -> 0%
where the time goes in v1:
time: 661 us; the launch traced here: 652 us
  waiting for transfers between devices  243 us (37%)
  matrix products  230 us (35%)
  starting transfers between devices  55.5 us (8%)
  blocking collectives  37.5 us (6%)
  loops' own time  31.3 us (5%)
  other arithmetic  20.9 us (3%)
  local copies, waits for them, and re-layouts  17.7 us (3%)
  between operations  15.4 us (2%)
    ppermute x3, waiting for transfers between devices, per_device(): recv = lax.ppermute(grad, 'stage', bwd_perm)  212 us
    dot_general x3, matrix products, per_device(): lax.dot_general(h_cols, du, CONTRACT_FIRST, preferred_element_type=jnp.fl...  78.3 us
    dot_general x6, matrix products, up_proj(): jnp.dot(h_in, w_one, preferred_element_type=jnp.float32)  73.7 us
    ppermute x3, starting transfers between devices, per_device(): recv = lax.ppermute(hidden, 'stage', fwd_perm)  49.8 us
    psum x1, blocking collectives, per_device(): total_loss = lax.psum(part_loss, ('stage', 'data'))  37.5 us
    dot_general x3, matrix products, per_device(): lax.dot_general(g, e_cols, CONTRACT_FIRST, preferred_element_type=jnp.flo...  33 us
    ppermute x3, waiting for transfers between devices, per_device(): recv = lax.ppermute(hidden, 'stage', fwd_perm)  29.5 us
    dot_general x2, matrix products, run_bwd(): lax.dot_general(du, w_up[layer], CONTRACT_LAST, preferred_element_type=jn...  26.8 us
  transfers between devices with their start and end apart: 18, of which 6 were waited for; matrix products, arithmetic and copies ran while one was open for 33% of the time, Pallas kernels for 0%

profile of v1, /device:TPU:0, one launch (start us, length us, event | category | flops | bytes accessed | tf_op | source)
XLA Modules:
  0.0 651.7 jit_solution(16855668556817205466)
XLA Ops:
  7.2 43.2 %conditional.8 = (bf16[256,896]{1,0:T(8,128)(2,1)S(1)}, bf16[256,896]{1,0:T(8,128)(2,1)S(1)}, bf16[256,896]{1,0:T(8,128)(2,1)}, bf16[256,896]{1,0:T(8,128)(2,1)}...) conditional(s32[]{:T(128)} %convert_element_type.472, ...), branch_computations={%region_0.0_spmd, %region_1.0_spmd} | conditional | flops 13431373824 | bytes 164364608 | solution.py:57
  8.3 6.5 fusion.18
  14.8 7.6 %fusion.85 = bf16[256,896]{1,0:T(8,128)(2,1)S(1)} fusion(bf16[3,4864,896]{2,1,0:T(8,128)(2,1)} %get-tuple-element.153, bf16[256,4864]{1,0:T(8,128)(2,1)S(1)} %fusion.18, bf16[256,896]{1,0:T(8,128)(2,1)S(1)} %copy-done.9), kind=kOutput, calls=%fused_computation.68 | convolution fusion | flops 2244509696 | bytes 12124160 | tf_op jit(solution)/shard_map/cond/branch_1_fun/dot_general | solution.py:53
  22.5 8.5 %fusion.21 = bf16[256,4864]{1,0:T(8,128)(2,1)} fusion(bf16[256,896]{1,0:T(8,128)(2,1)S(1)} %fusion.85, bf16[3,896,4864]{2,1,0:T(8,128)(2,1)} %get-tuple-element.152), kind=kOutput, calls=%fused_computation.31 | convolution fusion | flops 2232614912 | bytes 11665408 | tf_op jit(solution)/shard_map/cond/branch_1_fun/dot_general | solution.py:13
  31.0 5.7 fusion.80
  36.8 8.1 %fusion.24 = bf16[256,4864]{1,0:T(8,128)(2,1)} fusion(bf16[256,896]{1,0:T(8,128)(2,1)} %fusion.80, bf16[3,896,4864]{2,1,0:T(8,128)(2,1)} %get-tuple-element.152), kind=kOutput, calls=%fused_computation.32 | convolution fusion | flops 2232614912 | bytes 11665408 | tf_op jit(solution)/shard_map/cond/branch_1_fun/dot_general | solution.py:13
  44.9 5.0 fusion.75
  52.5 10.7 %collective-permute-done = bf16[256,896]{1,0:T(8,128)(2,1)S(1)} collective-permute-done((bf16[256,896]{1,0:T(8,128)(2,1)S(1)}, bf16[256,896]{1,0:T(8,128)(2,1)S(1)}, u32[]{:S(2)}, u32[]{:S(2)}) %collective-permute-start) | collective-permute-done | bytes 458784 | tf_op jit(solution)/shard_map/ppermute | solution.py:59
  63.3 4.6 conditional.9
  67.8 44.0 %collective-permute-start.1 = (bf16[256,896]{1,0:T(8,128)(2,1)S(1)}, bf16[256,896]{1,0:T(8,128)(2,1)S(1)}, u32[]{:S(2)}, u32[]{:S(2)}) collective-permute-start(bf16[256,896]{1,0:T(8,128)(2,1)S(1)} %get-tuple-element.239), channel_id=1, source_target_pairs={{0,8},{8,16},{16,24},{1,9},{9,17},{17,25},{2,10},{10,18},{18,26},{... | collective-permute-start | bytes 1376264 | tf_op jit(solution)/shard_map/ppermute | solution.py:59
  111.9 9.8 %collective-permute-done.1 = bf16[256,896]{1,0:T(8,128)(2,1)S(1)} collective-permute-done((bf16[256,896]{1,0:T(8,128)(2,1)S(1)}, bf16[256,896]{1,0:T(8,128)(2,1)S(1)}, u32[]{:S(2)}, u32[]{:S(2)}) %collective-permute-start.1) | collective-permute-done | bytes 458784 | tf_op jit(solution)/shard_map/ppermute | solution.py:59
  121.7 4.8 conditional.10
  126.6 4.4 collective-permute-start.2
  131.0 9.0 %collective-permute-done.2 = bf16[256,896]{1,0:T(8,128)(2,1)S(1)} collective-permute-done((bf16[256,896]{1,0:T(8,128)(2,1)S(1)}, bf16[256,896]{1,0:T(8,128)(2,1)S(1)}, u32[]{:S(2)}, u32[]{:S(2)}) %collective-permute-start.2) | collective-permute-done | bytes 458784 | tf_op jit(solution)/shard_map/ppermute | solution.py:59
  140.1 5.3 conditional.11
  147.0 1.9 multiply_convert_fusion
  148.9 6.9 %conditional.12 = (bf16[256,896]{1,0:T(8,128)(2,1)S(1)}, bf16[256,896]{1,0:T(8,128)(2,1)}, bf16[256,896]{1,0:T(8,128)(2,1)}, bf16[256,896]{1,0:T(8,128)(2,1)S(1)}) conditional(s32[]{:T(128)} %convert_element_type.469, bf16[256,896]{1,0:T(8,128)(2,1)S(1)} %get-tuple-element.294, (bf16[256,896]{1,0:T(8,128)(2,1)S(1)}, ...), branch_computations={%region_10.11_spmd, %region_11.12_spmd} | conditional | flops 13476200448 | bytes 74776640 | solution.py:82
  157.1 50.0 %collective-permute-done.3 = bf16[256,896]{1,0:T(8,128)(2,1)S(1)} collective-permute-done((bf16[256,896]{1,0:T(8,128)(2,1)S(1)}, bf16[256,896]{1,0:T(8,128)(2,1)S(1)}, u32[]{:S(2)}, u32[]{:S(2)}) %collective-permute-start.3) | collective-permute-done | bytes 458784 | tf_op jit(solution)/shard_map/ppermute | solution.py:84
  208.2 5.4 conditional.13
  214.9 11.7 %collective-permute-done.4 = bf16[256,896]{1,0:T(8,128)(2,1)S(1)} collective-permute-done((bf16[256,896]{1,0:T(8,128)(2,1)S(1)}, bf16[256,896]{1,0:T(8,128)(2,1)S(1)}, u32[]{:S(2)}, u32[]{:S(2)}) %collective-permute-start.4) | collective-permute-done | bytes 458784 | tf_op jit(solution)/shard_map/ppermute | solution.py:84
  226.7 5.3 conditional.14
  233.4 150.1 %collective-permute-done.5 = bf16[256,896]{1,0:T(8,128)(2,1)S(1)} collective-permute-done((bf16[256,896]{1,0:T(8,128)(2,1)S(1)}, bf16[256,896]{1,0:T(8,128)(2,1)S(1)}, u32[]{:S(2)}, u32[]{:S(2)}) %collective-permute-start.5) | collective-permute-done | bytes 458784 | tf_op jit(solution)/shard_map/ppermute | solution.py:84
  383.4 26.8 %conditional.15 = ((bf16[256,896]{1,0:T(8,128)(2,1)}, bf16[256,896]{1,0:T(8,128)(2,1)}, bf16[256,896]{1,0:T(8,128)(2,1)})) conditional(s32[]{:T(128)} %convert_element_type.472, (bf16[256,896]{1,0:T(8,128)(2,1)}, bf16[256,896]{1,0:T(8,128)(2,1)}, bf16[256,896]{1,0:T(8,128)(2,1)}) %tuple.83, (pred[]{:T(512)}, bf16[3,4864,896]{2,1,0:T(8,128)(2,1)}, ...), branch_computations={%region_16.17_spmd, %region_17.18_spmd} | conditional | flops 8984363008 | bytes 45809724 | solution.py:82
  383.5 12.1 %fusion.765 = bf16[256,896]{1,0:T(8,128)(2,1)} fusion(bf16[3,896,4864]{2,1,0:T(8,128)(2,1)} %get-tuple-element.184, bf16[256,4864]{1,0:T(8,128)(2,1)} %get-tuple-element.183, bf16[256,896]{1,0:T(8,128)(2,1)S(1)} %broadcast_select_fusion, bf16[3,4864,896]{2,1,0:T(8,128)(2,1)} %get-tuple-element.182), kind=kOutput, calls=%fused_computation.654 | convolution fusion | flops 4492066816 | bytes 21299200 | tf_op jit(solution)/shard_map/cond/branch_1_fun/dot_general | solution.py:78
  395.6 14.7 %fusion.762 = bf16[256,896]{1,0:T(8,128)(2,1)} fusion(bf16[3,896,4864]{2,1,0:T(8,128)(2,1)} %get-tuple-element.184, bf16[256,4864]{1,0:T(8,128)(2,1)} %get-tuple-element.185, bf16[256,896]{1,0:T(8,128)(2,1)} %fusion.765, bf16[3,4864,896]{2,1,0:T(8,128)(2,1)} %get-tuple-element.182), kind=kOutput, calls=%fused_computation.653 | convolution fusion | flops 4492066816 | bytes 21299200 | tf_op jit(solution)/shard_map/cond/branch_1_fun/dot_general | solution.py:78
  411.6 37.5 %psum.7 = f32[]{:T(128)} all-reduce(f32[]{:T(128)S(6)} %select_n.79), channel_id=1, replica_groups=mesh['stage'=4,'data'=8] {'stage','data'}, use_global_device_ids=true, to_apply=%region_9.10 | all-reduce | flops 1 | bytes 8 | tf_op jit(solution)/shard_map/psum | solution.py:65
  449.1 16.7 %convolution_convert_fusion.2 = bf16[1024,4864]{1,0:T(8,128)(2,1)} fusion(bf16[1024,896]{1,0:T(8,128)(2,1)} %all-gather.7.cloned.1.call-done, bf16[3,896,4864]{2,1,0:T(8,128)(2,1)} %param.22), kind=kOutput, calls=%fused_computation.734 | convolution fusion | flops 8930459648 | bytes 20512768 | tf_op jit(solution)/shard_map/dot_general | solution.py:13
  465.9 16.6 %convolution_convert_fusion.1 = bf16[1024,4864]{1,0:T(8,128)(2,1)} fusion(bf16[1024,896]{1,0:T(8,128)(2,1)} %all-gather.11.cloned.1.call-done, bf16[3,896,4864]{2,1,0:T(8,128)(2,1)} %param.22), kind=kOutput, calls=%fused_computation.733 | convolution fusion | flops 8930459648 | bytes 20512768 | tf_op jit(solution)/shard_map/dot_general | solution.py:13
  482.5 17.3 %convolution_convert_fusion = bf16[1024,4864]{1,0:T(8,128)(2,1)} fusion(bf16[1024,896]{1,0:T(8,128)(2,1)} %all-gather.15.cloned.1.call-done, bf16[3,896,4864]{2,1,0:T(8,128)(2,1)} %param.22), kind=kOutput, calls=%fused_computation.732 | convolution fusion | flops 8930459648 | bytes 20512768 | tf_op jit(solution)/shard_map/dot_general | solution.py:13
  499.8 10.9 %fusion.819 = f32[4864,224]{0,1:T(8,128)S(1)} fusion(bf16[1024,4864]{1,0:T(8,128)(2,1)} %convolution_convert_fusion.2, bf16[1024,896]{1,0:T(8,128)(2,1)} %all-gather.9.cloned.1.call-done, s32[]{:T(128)S(6)} %select_n.81), kind=kOutput, calls=%fused_computation.725 | convolution fusion | flops 2281177088 | bytes 14843908 | tf_op jit(solution)/shard_map/dot_general | solution.py:100
  510.7 2.0 copy-done
  512.9 26.0 %fusion.829 = f32[224,4864]{1,0:T(8,128)} fusion(bf16[1024,4864]{1,0:T(8,128)(2,1)} %convolution_convert_fusion.2, bf16[1024,896]{1,0:T(8,128)(2,1)} %all-gather.9.cloned.1.call-done, bf16[3,4864,896]{2,1,0:T(8,128)(2,1)} %param.23, bf16[1024,896]{1,0:T(8,128)(2,1)} %all-gather.7.cloned.1.call-done, s32[]{:T(128)S(6)} %select_n.81), kind=kOutput, calls=%fused_computation.730 | convolution fusion | flops 11271405568 | bytes 25395204 | tf_op jit(solution)/shard_map/dot_general | solution.py:99
  538.9 3.1 constant_dynamic-slice_fusion.5
  542.6 26.0 %fusion.825 = f32[224,4864]{1,0:T(8,128)} fusion(bf16[1024,4864]{1,0:T(8,128)(2,1)} %convolution_convert_fusion.1, bf16[1024,896]{1,0:T(8,128)(2,1)} %all-gather.13.cloned.1.call-done, bf16[3,4864,896]{2,1,0:T(8,128)(2,1)} %param.23, bf16[1024,896]{1,0:T(8,128)(2,1)} %all-gather.11.cloned.1.call-done, s32[]{:T(128)S(6)} %select_n.81), kind=kOutput, calls=%fused_computation.728 | convolution fusion | flops 11271405568 | bytes 25395204 | tf_op jit(solution)/shard_map/dot_general | solution.py:99
  568.6 3.1 constant_dynamic-slice_fusion.4
  571.7 10.9 %fusion.817 = f32[4864,224]{0,1:T(8,128)S(1)} fusion(bf16[1024,4864]{1,0:T(8,128)(2,1)} %convolution_convert_fusion.1, bf16[1024,896]{1,0:T(8,128)(2,1)} %all-gather.13.cloned.1.call-done, s32[]{:T(128)S(6)} %select_n.81), kind=kOutput, calls=%fused_computation.724 | convolution fusion | flops 2281177088 | bytes 14843908 | tf_op jit(solution)/shard_map/dot_general | solution.py:100
  582.7 2.1 copy-done.1
  584.8 1.5 constant_dynamic-slice_fusion.1
  586.7 26.2 %fusion.821 = f32[224,4864]{1,0:T(8,128)} fusion(bf16[1024,4864]{1,0:T(8,128)(2,1)} %convolution_convert_fusion, bf16[1024,896]{1,0:T(8,128)(2,1)} %all-gather.17.cloned.1.call-done, bf16[3,4864,896]{2,1,0:T(8,128)(2,1)} %param.23, bf16[1024,896]{1,0:T(8,128)(2,1)} %all-gather.15.cloned.1.call-done, s32[]{:T(128)S(6)} %select_n.81), kind=kOutput, calls=%fused_computation.726 | convolution fusion | flops 11271405568 | bytes 25395204 | tf_op jit(solution)/shard_map/dot_general | solution.py:99
  612.9 1.9 constant_dynamic-slice_fusion.3
  614.9 11.1 %fusion.815 = f32[4864,224]{0,1:T(8,128)S(1)} fusion(bf16[1024,4864]{1,0:T(8,128)(2,1)} %convolution_convert_fusion, bf16[1024,896]{1,0:T(8,128)(2,1)} %all-gather.17.cloned.1.call-done, s32[]{:T(128)S(6)} %select_n.81), kind=kOutput, calls=%fused_computation.723 | convolution fusion | flops 2281177088 | bytes 14843908 | tf_op jit(solution)/shard_map/dot_general | solution.py:100
  626.8 2.8 add_bitcast_fusion.5
  629.7 2.2 add_bitcast_fusion.2
  631.9 1.9 add_bitcast_fusion.4
  633.9 2.1 add_bitcast_fusion.3
  635.9 3.3 pad_maximum_fusion
  639.2 1.9 add_bitcast_fusion.1
  641.4 3.3 pad_maximum_fusion.1
  (101 shorter events, 14.6 us)
Async XLA Ops:
  7.2 442.0 %all-gather.7.cloned.1.call-start = ((), (), s32[]{:S(2)}) async-start(), calls=%async_computation | async-start | bytes 2293760 | tf_op jit(solution)/shard_map/all_gather | solution.py:68
  8.3 6.5 %copy-start.9 = (bf16[256,896]{1,0:T(8,128)(2,1)S(1)}, bf16[256,896]{1,0:T(8,128)(2,1)}, u32[]{:S(2)}) copy-start(bf16[256,896]{1,0:T(8,128)(2,1)} %get-tuple-element.304) | copy-start | bytes 1376260 | tf_op jit(solution)/shard_map/cond
  8.3 22.7 %slice-start.8 = ((s8[26148864]{0:T(1024)(128)(4,1)}), s8[4194304]{0:T(1024)(128)(4,1)S(1)}, s32[]{:S(2)}) async-start(s8[26148864]{0:T(1024)(128)(4,1)} %bitcast.397), calls=%async_computation.14 | async-start | bytes 8388608 | tf_op jit(solution)/shard_map/cond
  8.3 22.7 %slice-start.9 = ((s8[26148864]{0:T(1024)(128)(4,1)}), s8[4194304]{0:T(1024)(128)(4,1)S(1)}, s32[]{:S(2)}) async-start(s8[26148864]{0:T(1024)(128)(4,1)} %bitcast.397), calls=%async_computation.15 | async-start | bytes 8388608 | tf_op jit(solution)/shard_map/cond
  14.8 16.2 %copy-start.2 = (bf16[256,4864]{1,0:T(8,128)(2,1)}, bf16[256,4864]{1,0:T(8,128)(2,1)S(1)}, u32[]{:S(2)}) copy-start(bf16[256,4864]{1,0:T(8,128)(2,1)S(1)} %fusion.18) | copy-start | bytes 7471108 | tf_op jit(solution)/shard_map/cond
  14.8 16.2 %slice-start.10 = ((s8[26148864]{0:T(1024)(128)(4,1)}), s8[4194304]{0:T(1024)(128)(4,1)S(1)}, s32[]{:S(2)}) async-start(s8[26148864]{0:T(1024)(128)(4,1)} %bitcast.397), calls=%async_computation.16 | async-start | bytes 8388608 | tf_op jit(solution)/shard_map/cond
  14.8 16.2 %slice-start.11 = ((s8[26148864]{0:T(1024)(128)(4,1)}), s8[4194304]{0:T(1024)(128)(4,1)S(1)}, s32[]{:S(2)}) async-start(s8[26148864]{0:T(1024)(128)(4,1)} %bitcast.397), calls=%async_computation.17 | async-start | bytes 8388608 | tf_op jit(solution)/shard_map/cond
  14.8 16.2 %slice-start.12 = ((s8[26148864]{0:T(1024)(128)(4,1)}), s8[4194304]{0:T(1024)(128)(4,1)S(1)}, s32[]{:S(2)}) async-start(s8[26148864]{0:T(1024)(128)(4,1)} %bitcast.397), calls=%async_computation.18 | async-start | bytes 8388608 | tf_op jit(solution)/shard_map/cond
  14.8 16.2 %slice-start.13 = ((s8[26148864]{0:T(1024)(128)(4,1)}), s8[4194304]{0:T(1024)(128)(4,1)S(1)}, s32[]{:S(2)}) async-start(s8[26148864]{0:T(1024)(128)(4,1)} %bitcast.397), calls=%async_computation.19 | async-start | bytes 8388608 | tf_op jit(solution)/shard_map/cond
  22.5 14.3 %copy-start.10 = (bf16[256,896]{1,0:T(8,128)(2,1)}, bf16[256,896]{1,0:T(8,128)(2,1)S(1)}, u32[]{:S(2)}) copy-start(bf16[256,896]{1,0:T(8,128)(2,1)S(1)} %fusion.85) | copy-start | bytes 1376260 | tf_op jit(solution)/shard_map/cond
  22.5 8.5 %slice-start.14 = ((s8[26148864]{0:T(1024)(128)(4,1)}), s8[983040]{0:T(1024)(128)(4,1)S(1)}, s32[]{:S(2)}) async-start(s8[26148864]{0:T(1024)(128)(4,1)} %bitcast.397), calls=%async_computation.20 | async-start | bytes 1966080 | tf_op jit(solution)/shard_map/cond
  50.4 0.8 copy-start.14
  51.2 12.0 %collective-permute-start = (bf16[256,896]{1,0:T(8,128)(2,1)S(1)}, bf16[256,896]{1,0:T(8,128)(2,1)S(1)}, u32[]{:S(2)}, u32[]{:S(2)}) collective-permute-start(bf16[256,896]{1,0:T(8,128)(2,1)S(1)} %get-tuple-element.232), channel_id=1, source_target_pairs={{0,8},{8,16},{16,24},{1,9},{9,17},{17,25},{2,10},{10,18},{18,26},{... | collective-permute-start | bytes 1376264 | tf_op jit(solution)/shard_map/ppermute | solution.py:59
  67.8 53.9 %collective-permute-start.1 = (bf16[256,896]{1,0:T(8,128)(2,1)S(1)}, bf16[256,896]{1,0:T(8,128)(2,1)S(1)}, u32[]{:S(2)}, u32[]{:S(2)}) collective-permute-start(bf16[256,896]{1,0:T(8,128)(2,1)S(1)} %get-tuple-element.239), channel_id=1, source_target_pairs={{0,8},{8,16},{16,24},{1,9},{9,17},{17,25},{2,10},{10,18},{18,26},{... | collective-permute-start | bytes 1376264 | tf_op jit(solution)/shard_map/ppermute | solution.py:59
  126.6 13.4 %collective-permute-start.2 = (bf16[256,896]{1,0:T(8,128)(2,1)S(1)}, bf16[256,896]{1,0:T(8,128)(2,1)S(1)}, u32[]{:S(2)}, u32[]{:S(2)}) collective-permute-start(bf16[256,896]{1,0:T(8,128)(2,1)S(1)} %get-tuple-element.252), channel_id=1, source_target_pairs={{0,8},{8,16},{16,24},{1,9},{9,17},{17,25},{2,10},{10,18},{18,26},{... | collective-permute-start | bytes 1376264 | tf_op jit(solution)/shard_map/ppermute | solution.py:59
  145.4 320.5 %all-gather.11.cloned.1.call-start = ((), (), s32[]{:S(2)}) async-start(), calls=%async_computation.2 | async-start | bytes 2293760 | tf_op jit(solution)/shard_map/all_gather | solution.py:68
  146.2 336.3 %all-gather.15.cloned.1.call-start = ((), (), s32[]{:S(2)}) async-start(), calls=%async_computation.4 | async-start | bytes 2293760 | tf_op jit(solution)/shard_map/all_gather | solution.py:68
  146.9 352.9 %all-gather.9.cloned.1.call-start = ((), (), s32[]{:S(2)}) async-start(), calls=%async_computation.1 | async-start | bytes 2293760 | tf_op jit(solution)/shard_map/all_gather | solution.py:87
  155.8 1.3 copy-start.15
  155.8 1.3 copy-start.16
  155.8 51.3 %collective-permute-start.3 = (bf16[256,896]{1,0:T(8,128)(2,1)S(1)}, bf16[256,896]{1,0:T(8,128)(2,1)S(1)}, u32[]{:S(2)}, u32[]{:S(2)}) collective-permute-start(bf16[256,896]{1,0:T(8,128)(2,1)S(1)} %get-tuple-element.258), channel_id=1, source_target_pairs={{8,0},{16,8},{24,16},{9,1},{17,9},{25,17},{10,2},{18,10},{26,18},{... | collective-permute-start | bytes 1376264 | tf_op jit(solution)/shard_map/ppermute | solution.py:84
  213.6 13.0 %collective-permute-start.4 = (bf16[256,896]{1,0:T(8,128)(2,1)S(1)}, bf16[256,896]{1,0:T(8,128)(2,1)S(1)}, u32[]{:S(2)}, u32[]{:S(2)}) collective-permute-start(bf16[256,896]{1,0:T(8,128)(2,1)S(1)} %get-tuple-element.262), channel_id=1, source_target_pairs={{8,0},{16,8},{24,16},{9,1},{17,9},{25,17},{10,2},{18,10},{26,18},{... | collective-permute-start | bytes 1376264 | tf_op jit(solution)/shard_map/ppermute | solution.py:84
  232.1 151.4 %collective-permute-start.5 = (bf16[256,896]{1,0:T(8,128)(2,1)S(1)}, bf16[256,896]{1,0:T(8,128)(2,1)S(1)}, u32[]{:S(2)}, u32[]{:S(2)}) collective-permute-start(bf16[256,896]{1,0:T(8,128)(2,1)S(1)} %get-tuple-element.269), channel_id=1, source_target_pairs={{8,0},{16,8},{24,16},{9,1},{17,9},{25,17},{10,2},{18,10},{26,18},{... | collective-permute-start | bytes 1376264 | tf_op jit(solution)/shard_map/ppermute | solution.py:84
  383.5 12.1 %copy-start.17 = (bf16[256,896]{1,0:T(8,128)(2,1)}, bf16[256,896]{1,0:T(8,128)(2,1)S(1)}, u32[]{:S(2)}) copy-start(bf16[256,896]{1,0:T(8,128)(2,1)S(1)} %broadcast_select_fusion) | copy-start | bytes 1376260 | tf_op jit(solution)/shard_map/cond
  410.3 132.3 %all-gather.13.cloned.1.call-start = ((), (), s32[]{:S(2)}) async-start(), calls=%async_computation.3 | async-start | bytes 2293760 | tf_op jit(solution)/shard_map/all_gather | solution.py:87
  410.9 175.9 %all-gather.17.cloned.1.call-start = ((), (), s32[]{:S(2)}) async-start(), calls=%async_computation.5 | async-start | bytes 2293760 | tf_op jit(solution)/shard_map/all_gather | solution.py:87
  510.7 2.0 copy-start
  542.1 84.2 %collective-permute-start.6 = (f32[112,4864]{1,0:T(8,128)}, f32[112,4864]{1,0:T(8,128)}, u32[]{:S(2)}, u32[]{:S(2)}) collective-permute-start(f32[112,4864]{1,0:T(8,128)} %constant_dynamic-slice_fusion.5), channel_id=1, source_target_pairs={{0,1},{1,0},{2,3},{3,2},{4,5},{5,4},{6,7},{7,6},{8,9},{9,8},{10,11... | collective-permute-start | bytes 6537224 | tf_op jit(solution)/shard_map/ppermute | solution.py:105
  542.1 87.6 %collective-permute-start.9 = (f32[4864,112]{0,1:T(8,128)S(1)}, f32[4864,112]{0,1:T(8,128)}, u32[]{:S(2)}, u32[]{:S(2)}) collective-permute-start(f32[4864,112]{0,1:T(8,128)S(1)} %constant_dynamic-slice_fusion.2), channel_id=1, source_target_pairs={{0,1},{1,0},{2,3},{3,2},{4,5},{5,4},{6,7},{7,6},{8,9},{9,8},{10,11... | collective-permute-start | bytes 6537224 | tf_op jit(solution)/shard_map/ppermute | solution.py:106
  571.7 60.2 %collective-permute-start.7 = (f32[112,4864]{1,0:T(8,128)}, f32[112,4864]{1,0:T(8,128)}, u32[]{:S(2)}, u32[]{:S(2)}) collective-permute-start(f32[112,4864]{1,0:T(8,128)} %constant_dynamic-slice_fusion.4), channel_id=1, source_target_pairs={{0,1},{1,0},{2,3},{3,2},{4,5},{5,4},{6,7},{7,6},{8,9},{9,8},{10,11... | collective-permute-start | bytes 6537224 | tf_op jit(solution)/shard_map/ppermute | solution.py:105
  582.7 2.1 copy-start.1
  586.2 53.0 %collective-permute-start.10 = (f32[4864,112]{0,1:T(8,128)}, f32[4864,112]{0,1:T(8,128)}, u32[]{:S(2)}, u32[]{:S(2)}) collective-permute-start(f32[4864,112]{0,1:T(8,128)} %constant_dynamic-slice_fusion.1), channel_id=1, source_target_pairs={{0,1},{1,0},{2,3},{3,2},{4,5},{5,4},{6,7},{7,6},{8,9},{9,8},{10,11... | collective-permute-start | bytes 6537224 | tf_op jit(solution)/shard_map/ppermute | solution.py:106
  612.9 16.7 %slice-start = ((s8[4358144]{0:T(1024)(128)(4,1)}), s8[4194304]{0:T(1024)(128)(4,1)S(1)}, s32[]{:S(2)}) async-start(s8[4358144]{0:T(1024)(128)(4,1)} %bitcast.387), calls=%async_computation.6 | async-start | bytes 8388608
  614.8 14.8 %slice-start.1 = ((s8[4358144]{0:T(1024)(128)(4,1)}), s8[163840]{0:T(1024)(128)(4,1)S(1)}, s32[]{:S(2)}) async-start(s8[4358144]{0:T(1024)(128)(4,1)} %bitcast.387), calls=%async_computation.7 | async-start | bytes 327680
  614.9 19.0 %collective-permute-start.8 = (f32[112,4864]{1,0:T(8,128)S(1)}, f32[112,4864]{1,0:T(8,128)}, u32[]{:S(2)}, u32[]{:S(2)}) collective-permute-start(f32[112,4864]{1,0:T(8,128)S(1)} %constant_dynamic-slice_fusion.3), channel_id=1, source_target_pairs={{0,1},{1,0},{2,3},{3,2},{4,5},{5,4},{6,7},{7,6},{8,9},{9,8},{10,11... | collective-permute-start | bytes 6537224 | tf_op jit(solution)/shard_map/ppermute | solution.py:105
  626.1 5.8 slice-start.4
  626.3 5.6 slice-start.5
  626.3 14.9 %collective-permute-start.11 = (f32[4864,112]{0,1:T(8,128)S(1)}, f32[4864,112]{0,1:T(8,128)S(1)}, u32[]{:S(2)}, u32[]{:S(2)}) collective-permute-start(f32[4864,112]{0,1:T(8,128)S(1)} %constant_dynamic-slice_fusion), channel_id=1, source_target_pairs={{0,1},{1,0},{2,3},{3,2},{4,5},{5,4},{6,7},{7,6},{8,9},{9,8},{10,11... | collective-permute-start | bytes 6537224 | tf_op jit(solution)/shard_map/ppermute | solution.py:106
  626.8 7.0 %slice-start.6 = ((s8[4358144]{0:T(1024)(128)(4,1)}), s8[4194304]{0:T(1024)(128)(4,1)S(1)}, s32[]{:S(2)}) async-start(s8[4358144]{0:T(1024)(128)(4,1)} %bitcast.393), calls=%async_computation.12 | async-start | bytes 8388608
  629.7 4.2 slice-start.7
  633.9 5.4 slice-start.2
  635.9 3.3 slice-start.3
Sparse Core Ops, SparseCore 0:
  145.5 110.5 all-gather.6
  258.0 32.7 all-gather.10
  292.6 32.7 all-gather.14
  410.4 28.6 all-gather.8
  440.8 32.7 all-gather.12
  475.3 32.7 all-gather.16

commit v2 on v1

v2 whole, which is shorter than its diff:
```python
import functools

import jax
import jax.numpy as jnp
from jax import lax
from jax.experimental import pallas as pl
from jax.experimental.pallas import tpu as pltpu
from jax.sharding import PartitionSpec as P

CONTRACT_LAST = (((1,), (1,)), ((), ()))
CONTRACT_FIRST = (((0,), (0,)), ((), ()))
SAME_CORE = [[0, 2, 4, 6], [1, 3, 5, 7]]
SWAP_CORE = [(0, 1), (1, 0), (2, 3), (3, 2), (4, 5), (5, 4), (6, 7), (7, 6)]
MESH = pl.DeviceIdType.MESH
GELU_C = 0.7978845608028654
GELU_A = 0.044715
CHIPS = 4


def up_proj(h_in, w_one):
    return jnp.dot(h_in, w_one, preferred_element_type=jnp.float32).astype(jnp.bfloat16)


def gelu_of(pre_act):
    return jax.nn.gelu(pre_act.astype(jnp.float32)).astype(jnp.bfloat16)


def grad_pre_of(grad_out, pre_act, w_two):
    grad_act = lax.dot_general(grad_out, w_two, CONTRACT_LAST, preferred_element_type=jnp.float32).astype(jnp.bfloat16)
    return jax.jvp(jax.nn.gelu, (pre_act.astype(jnp.float32),), (grad_act.astype(jnp.float32),))[1].astype(jnp.bfloat16)


def gelu_wide(u):
    th = jnp.tanh(u * (GELU_C + (GELU_C * GELU_A) * (u * u)))
    return u * (0.5 + 0.5 * th)


def gelu_slope(u):
    sq = u * u
    th = jnp.tanh(u * (GELU_C + (GELU_C * GELU_A) * sq))
    half = 0.5 + 0.5 * th
    return half + (0.5 * u) * (1.0 - th * th) * (GELU_C + (3.0 * GELU_C * GELU_A) * sq)


def chain_kernel(stages, total_tokens, x_ref, y_ref, w1_hbm, w2_hbm, h_all, e_out, loss_ref,
                 w1, w2, ut, g_buf, hs, e_t, e_nat, y_buf,
                 w1_sem, w2_sem, io_sem, hop_send, hop_recv, ag_send, ag_recv):
    stage = lax.axis_index('stage')
    data = lax.axis_index('data')
    chip = data // 2
    core = data % 2
    n_layers, width, ffn = w1.shape
    not_first = stage > 0
    not_last = stage < stages - 1

    def load_w1(l):
        return pltpu.make_async_copy(w1_hbm.at[l], w1.at[l], w1_sem.at[l])

    def load_w2(l, s):
        return pltpu.make_async_copy(w2_hbm.at[l], w2.at[l % 2], w2_sem.at[s])

    x_copy = pltpu.make_async_copy(x_ref, hs.at[0], io_sem.at[0])
    y_copy = pltpu.make_async_copy(y_ref, y_buf, io_sem.at[1])

    @pl.when(jnp.logical_not(not_first))
    def _():
        x_copy.start()

    load_w1(0).start()
    load_w2(0, 0).start()
    load_w1(1).start()
    load_w2(1, 1).start()
    load_w1(2).start()

    @pl.when(jnp.logical_not(not_last))
    def _():
        y_copy.start()

    peers = []
    for j in range(1, CHIPS):
        px = (chip // 2 + j // 2) % 2
        py = (chip % 2 + j % 2) % 2
        peers.append((px * 2 + py) * 2 + core)

    barrier = pltpu.get_barrier_semaphore()
    for p in peers:
        pl.semaphore_signal(barrier, inc=1, device_id=(stage, p), device_id_type=MESH)

    @pl.when(not_first)
    def _():
        pl.semaphore_signal(barrier, inc=1, device_id=(stage - 1, data), device_id_type=MESH)

    @pl.when(not_last)
    def _():
        pl.semaphore_signal(barrier, inc=1, device_id=(stage + 1, data), device_id_type=MESH)

    pl.semaphore_wait(barrier, CHIPS - 1 + jnp.minimum(stage, 1) + jnp.minimum(stages - 1 - stage, 1))

    def hop_up():
        return pltpu.make_async_remote_copy(
            src_ref=hs.at[n_layers], dst_ref=hs.at[0], send_sem=hop_send.at[0], recv_sem=hop_recv.at[0],
            device_id=(stage + 1, data), device_id_type=MESH)

    def hop_down():
        return pltpu.make_async_remote_copy(
            src_ref=e_t.at[0], dst_ref=e_t.at[n_layers], send_sem=hop_send.at[1], recv_sem=hop_recv.at[1],
            device_id=(stage - 1, data), device_id_type=MESH)

    def gather(l, j):
        return pltpu.make_async_remote_copy(
            src_ref=hs.at[l], dst_ref=h_all.at[l, chip], send_sem=ag_send.at[l, j], recv_sem=ag_recv.at[l, j],
            device_id=(stage, peers[j]), device_id_type=MESH)

    def keep(l):
        return pltpu.make_async_copy(hs.at[l], h_all.at[l, chip], io_sem.at[2 + l])

    @pl.when(not_first)
    def _():
        hop_up().wait_recv()

    @pl.when(jnp.logical_not(not_first))
    def _():
        x_copy.wait()

    def fwd_layer(l, carry):
        for j in range(CHIPS - 1):
            gather(l, j).start()
        keep(l).start()
        load_w1(l).wait()
        h = hs[l]
        for c in range(ffn // 256):
            cols = slice(c * 256, (c + 1) * 256)
            u = jnp.dot(h, w1[l, :, cols], preferred_element_type=jnp.float32).astype(jnp.bfloat16)
            ut[l, cols, :] = u.T
            g_buf[:, cols] = gelu_wide(u.astype(jnp.float32)).astype(jnp.bfloat16)
        load_w2(l, l).wait()
        branch = jnp.dot(g_buf[...], w2[l % 2], preferred_element_type=jnp.float32)
        hs[l + 1] = (h.astype(jnp.float32) + branch).astype(jnp.bfloat16)

        @pl.when(l == 0)
        def _():
            load_w2(2, 2).start()
        return carry

    lax.fori_loop(0, n_layers, fwd_layer, 0)

    @pl.when(not_last)
    def _():
        hop_up().start()
        loss_ref[...] = jnp.zeros_like(loss_ref)
        hop_up().wait_send()
        hop_down().wait_recv()

    @pl.when(jnp.logical_not(not_last))
    def _():
        y_copy.wait()
        diff = hs[n_layers].astype(jnp.float32) - y_buf[...].astype(jnp.float32)
        loss_ref[...] = jnp.sum(diff * diff, axis=0, keepdims=True)
        e_t[n_layers] = (diff / total_tokens).T.astype(jnp.bfloat16)

    rows_c = ffn // 4

    def bwd_layer(i, carry):
        l = n_layers - 1 - i

        @pl.when(l == 0)
        def _():
            load_w2(0, 3).wait()
        e_cur = e_t[l + 1]
        for c in range(4):
            rows = slice(c * rows_c, (c + 1) * rows_c)
            dg = jnp.dot(w2[l % 2, rows, :], e_cur, preferred_element_type=jnp.float32).astype(jnp.bfloat16)
            slope = gelu_slope(ut[l, rows, :].astype(jnp.float32))
            ut[l, rows, :] = (dg.astype(jnp.float32) * slope).astype(jnp.bfloat16)

        @pl.when(l == 2)
        def _():
            load_w2(0, 3).start()

        @pl.when(jnp.logical_or(not_first, l > 0))
        def _():
            back = jnp.dot(w1[l], ut[l], preferred_element_type=jnp.float32)
            e_t[l] = (e_cur.astype(jnp.float32) + back).astype(jnp.bfloat16)
        return carry

    lax.fori_loop(0, n_layers, bwd_layer, 0)

    @pl.when(not_first)
    def _():
        hop_down().start()

    for l in range(n_layers):
        e_nat[l] = e_t[l + 1].T
        pltpu.make_async_copy(e_nat.at[l], e_out.at[l], io_sem.at[5 + l]).start()
    for l in range(n_layers):
        pltpu.make_async_copy(e_nat.at[l], e_out.at[l], io_sem.at[5 + l]).wait()
        keep(l).wait()
        for j in range(CHIPS - 1):
            gather(l, j).wait_send()
            gather(l, j).wait_recv()

    @pl.when(not_first)
    def _():
        hop_down().wait_send()


def run_chain(x_rows, y_rows, w_up, w_down, stages, total_tokens):
    rows, width = x_rows.shape
    n_layers, _, ffn = w_up.shape
    bf = jnp.bfloat16
    any_spec = pl.BlockSpec(memory_space=pl.ANY)
    return pl.pallas_call(
        functools.partial(chain_kernel, stages, total_tokens),
        out_shape=(
            jax.ShapeDtypeStruct((n_layers, CHIPS, rows, width), bf),
            jax.ShapeDtypeStruct((n_layers, rows, width), bf),
            jax.ShapeDtypeStruct((1, width), jnp.float32),
        ),
        in_specs=[any_spec] * 4,
        out_specs=(any_spec, any_spec, pl.BlockSpec(memory_space=pltpu.VMEM)),
        scratch_shapes=[
            pltpu.VMEM((n_layers, width, ffn), bf),
            pltpu.VMEM((2, ffn, width), bf),
            pltpu.VMEM((n_layers, ffn, rows), bf),
            pltpu.VMEM((rows, ffn), bf),
            pltpu.VMEM((n_layers + 1, rows, width), bf),
            pltpu.VMEM((n_layers + 1, width, rows), bf),
            pltpu.VMEM((n_layers, rows, width), bf),
            pltpu.VMEM((rows, width), bf),
            pltpu.SemaphoreType.DMA((3,)),
            pltpu.SemaphoreType.DMA((4,)),
            pltpu.SemaphoreType.DMA((8,)),
            pltpu.SemaphoreType.DMA((2,)),
            pltpu.SemaphoreType.DMA((2,)),
            pltpu.SemaphoreType.DMA((3, 3)),
            pltpu.SemaphoreType.DMA((3, 3)),
        ],
        compiler_params=pltpu.CompilerParams(collective_id=0, has_side_effects=True, vmem_limit_bytes=67043328),
    )(x_rows, y_rows, w_up, w_down)


def solution(mesh):
    stages = mesh.shape['stage']
    replicas = mesh.shape['data']

    def per_device(x_loc, y_loc, w_up, w_down):
        n_micro, n_tokens, n_width = x_loc.shape
        n_layers = w_up.shape[0]
        rows = n_micro * n_tokens
        total_tokens = replicas * rows
        data_idx = lax.axis_index('data')
        x_rows = x_loc.reshape(rows, n_width)
        y_rows = y_loc.reshape(rows, n_width)
        h_gath, e_saved, loss_part = run_chain(x_rows, y_rows, w_up, w_down, stages, total_tokens)
        total_loss = lax.psum(jnp.sum(loss_part) / (2 * total_tokens), ('stage', 'data'))
        h_all = [h_gath[layer].reshape(CHIPS * rows, n_width) for layer in range(n_layers)]
        e_all = [lax.all_gather(e_saved[layer], 'data', axis_index_groups=SAME_CORE, tiled=True) for layer in range(n_layers)]

        chip = data_idx // 2
        core = data_idx % 2
        width_blk = n_width // replicas
        up_out, down_out = [], []
        for layer in range(n_layers):
            u = up_proj(h_all[layer], w_up[layer])
            g = gelu_of(u)
            du = grad_pre_of(e_all[layer], u, w_down[layer])
            h_cols = lax.dynamic_slice_in_dim(h_all[layer], chip * 2 * width_blk, 2 * width_blk, 1)
            e_cols = lax.dynamic_slice_in_dim(e_all[layer], chip * 2 * width_blk, 2 * width_blk, 1)
            g_one = lax.dot_general(h_cols, du, CONTRACT_FIRST, preferred_element_type=jnp.float32)
            g_two = lax.dot_general(g, e_cols, CONTRACT_FIRST, preferred_element_type=jnp.float32)
            send_one = lax.dynamic_slice_in_dim(g_one, (1 - core) * width_blk, width_blk, 0)
            keep_one = lax.dynamic_slice_in_dim(g_one, core * width_blk, width_blk, 0)
            send_two = lax.dynamic_slice_in_dim(g_two, (1 - core) * width_blk, width_blk, 1)
            keep_two = lax.dynamic_slice_in_dim(g_two, core * width_blk, width_blk, 1)
            up_out.append(keep_one + lax.ppermute(send_one, 'data', SWAP_CORE))
            down_out.append(keep_two + lax.ppermute(send_two, 'data', SWAP_CORE))
        return total_loss, jnp.stack(up_out), jnp.stack(down_out)

    return jax.shard_map(
        per_device,
        mesh=mesh,
        in_specs=(P('data', None, None), P('data', None, None), P('stage', None, None), P('stage', None, None)),
        out_specs=(P(), P('stage', 'data', None), P('stage', None, 'data')),
        check_vma=False,
    )
```

time: 661 us -> 488 us (0.74)
  waiting for transfers between devices: 243 us -> 1.41 us
  Pallas kernels: 0 us -> 228 us
  matrix products: 230 us -> 162 us
  starting transfers between devices: 55.5 us -> 1.76 us
  loops' own time: 31.3 us -> 0 us
    ppermute x6 -> x0, waiting for transfers between devices: 241 us -> none  [the longest x3 212 us: per_device(): recv = lax.ppermute(grad, 'stage', bwd_perm)]
    pallas_call x0 -> x1, Pallas kernels: none -> 228 us  [run_chain(): pl.pallas_call(functools.partial(chain_kernel, stages, total_tokens), out...]
    ppermute x6 -> x0, starting transfers between devices: 53.6 us -> none  [the longest x3 49.8 us: per_device(): recv = lax.ppermute(hidden, 'stage', fwd_perm)]
    dot_general x5 -> x0, matrix products: 45.1 us -> none  [the longest x2 26.8 us: run_bwd(): lax.dot_general(du, w_up[layer], CONTRACT_LAST, preferred_element_type=jn...]
    another operation x8 -> x0, loops' own time: 31.3 us -> none  [the longest x4 15.9 us: per_device(): lax.cond(stage_idx == tick, run_bwd, lambda ops: ops, (grad, e_saved))]
    dot_general x6 -> x3, matrix products: 73.7 us -> 50.4 us  [up_proj(): jnp.dot(h_in, w_one, preferred_element_type=jnp.float32)]
  transfers between devices with their start and end apart: 18 -> 9, of which waited for: 6 -> 0; matrix products, arithmetic and copies ran while one was open for 33% -> 39% of each run, Pallas kernels for 0% -> 0%
where the time goes in v2:
time: 488 us; the launch traced here: 483 us
  Pallas kernels  228 us (47%)
  matrix products  162 us (33%)
  blocking collectives  38.3 us (8%)
  local copies, waits for them, and re-layouts  19.7 us (4%)
  other arithmetic  17.1 us (4%)
  between operations  15 us (3%)
    pallas_call x1, Pallas kernels, run_chain(): pl.pallas_call(functools.partial(chain_kernel, stages, total_tokens), out...  228 us
    dot_general x3, matrix products, per_device(): lax.dot_general(h_cols, du, CONTRACT_FIRST, preferred_element_type=jnp.fl...  78.3 us
    dot_general x3, matrix products, up_proj(): jnp.dot(h_in, w_one, preferred_element_type=jnp.float32)  50.4 us
    psum x1, blocking collectives, per_device(): lax.psum(jnp.sum(loss_part) / (2 * total_tokens), ('stage', 'data'))  38.3 us
    dot_general x3, matrix products, per_device(): lax.dot_general(g, e_cols, CONTRACT_FIRST, preferred_element_type=jnp.flo...  33.1 us
    another operation x8, other arithmetic, per_device(): return (total_loss, jnp.stack(up_out), jnp.stack(down_out))  15.8 us
  transfers between devices with their start and end apart: 9, of which 0 were waited for; matrix products, arithmetic and copies ran while one was open for 39% of the time, Pallas kernels for 0%

profile of v2, /device:TPU:0, one launch (start us, length us, event | category | flops | bytes accessed | tf_op | source)
XLA Modules:
  0.0 482.5 jit_solution(2824533474451668012)
XLA Ops:
  7.2 0.0 all-gather.11.cloned.1.call-start
  7.2 227.6 %shard_map.67 = (bf16[3,4,256,896]{3,2,1,0:T(8,128)(2,1)}, bf16[3,256,896]{2,1,0:T(8,128)(2,1)}, f32[1,896]{1,0:T(1,128)}) custom-call(bf16[256,896]{1,0:T(8,128)(2,1)} %bitcast.76, bf16[256,896]{1,0:T(8,128)(2,1)} %bitcast.77, bf16[3,896,4864]{2,1,0:T(8,128)(2,1)} %w1_hbm.1, bf16[3,4864,896]{2,1,0:T(8,128)(2,1)} %w2_hbm.1), custom_call_target="tpu_custom_call" | custom-call | tf_op jit(solution)/shard_map/pallas_call | solution.py:212
  234.8 2.4 fusion.118
  237.2 0.0 all-gather.11.cloned.1.call-update
  237.2 0.0 all-gather.7.cloned.1.call-start
  237.3 0.7 all-gather.7.cloned.1.call-update
  238.0 0.0 all-gather.9.cloned.1.call-start
  238.0 0.7 all-gather.9.cloned.1.call-update
  238.7 1.3 reduce_sum.9
  240.7 38.3 %psum.7 = f32[]{:T(128)} all-reduce(f32[]{:T(128)S(6)} %div.11), channel_id=1, replica_groups=mesh['stage'=4,'data'=8] {'stage','data'}, use_global_device_ids=true, to_apply=%region_1.0 | all-reduce | flops 1 | bytes 8 | tf_op jit(solution)/shard_map/psum | solution.py:255
  279.0 3.1 fusion.117
  282.1 0.0 copy-start.4
  282.2 18.2 %convolution_convert_fusion = bf16[1024,4864]{1,0:T(8,128)(2,1)} fusion(bf16[1024,896]{1,0:T(8,128)(2,1)S(1)} %bitcast.74, bf16[3,896,4864]{2,1,0:T(8,128)(2,1)} %w1_hbm.1), kind=kOutput, calls=%fused_computation.66 | convolution fusion | flops 8930459648 | bytes 20512768 | tf_op jit(solution)/shard_map/dot_general | solution.py:21
  300.4 16.1 %convolution_convert_fusion.2 = bf16[1024,4864]{1,0:T(8,128)(2,1)} fusion(bf16[1024,896]{1,0:T(8,128)(2,1)S(1)} %bitcast.72, bf16[3,896,4864]{2,1,0:T(8,128)(2,1)} %w1_hbm.1), kind=kOutput, calls=%fused_computation.68 | convolution fusion | flops 8930459648 | bytes 20512768 | tf_op jit(solution)/shard_map/dot_general | solution.py:21
  316.4 16.1 %convolution_convert_fusion.1 = bf16[1024,4864]{1,0:T(8,128)(2,1)} fusion(bf16[1024,896]{1,0:T(8,128)(2,1)S(1)} %bitcast.70, bf16[3,896,4864]{2,1,0:T(8,128)(2,1)} %w1_hbm.1), kind=kOutput, calls=%fused_computation.67 | convolution fusion | flops 8930459648 | bytes 20512768 | tf_op jit(solution)/shard_map/dot_general | solution.py:21
  332.5 10.9 %fusion.33 = f32[4864,224]{0,1:T(8,128)S(1)} fusion(bf16[1024,4864]{1,0:T(8,128)(2,1)} %convolution_convert_fusion, bf16[1,1024,896]{2,1,0:T(8,128)(2,1)} %all-gather.11.cloned.1.call-done, s32[]{:T(128)S(6)} %select_n.18), kind=kOutput, calls=%fused_computation.57 | convolution fusion | flops 2281177088 | bytes 14843908 | tf_op jit(solution)/shard_map/dot_general | solution.py:270
  343.5 2.1 copy-done
  345.6 0.1 constant_dynamic-slice_fusion
  345.7 26.2 %fusion.39 = f32[224,4864]{1,0:T(8,128)} fusion(bf16[1024,4864]{1,0:T(8,128)(2,1)} %convolution_convert_fusion, bf16[3,4864,896]{2,1,0:T(8,128)(2,1)} %w2_hbm.1, bf16[1,1024,896]{2,1,0:T(8,128)(2,1)} %all-gather.11.cloned.1.call-done, bf16[1024,896]{1,0:T(8,128)(2,1)} %bitcast.75, s32[]{:T(128)S(6)} %select_n.18), kind=kOutput, calls=%fused_computation.60 | convolution fusion | flops 11271405568 | bytes 25395204 | tf_op jit(solution)/shard_map/dot_general | solution.py:269
  372.0 3.1 constant_dynamic-slice_fusion.3
  375.1 0.0 collective-permute-start.2
  375.1 0.5 collective-permute-start.5
  375.6 26.0 %fusion.47 = f32[224,4864]{1,0:T(8,128)} fusion(bf16[1024,4864]{1,0:T(8,128)(2,1)} %convolution_convert_fusion.2, bf16[3,4864,896]{2,1,0:T(8,128)(2,1)} %w2_hbm.1, bf16[1,1024,896]{2,1,0:T(8,128)(2,1)} %all-gather.7.cloned.1.call-done, bf16[1024,896]{1,0:T(8,128)(2,1)} %bitcast.73, s32[]{:T(128)S(6)} %select_n.18), kind=kOutput, calls=%fused_computation.64 | convolution fusion | flops 11271405568 | bytes 25395204 | tf_op jit(solution)/shard_map/dot_general | solution.py:269
  401.6 3.1 constant_dynamic-slice_fusion.5
  404.7 0.0 collective-permute-start
  404.7 10.9 %fusion.37 = f32[4864,224]{0,1:T(8,128)S(1)} fusion(bf16[1024,4864]{1,0:T(8,128)(2,1)} %convolution_convert_fusion.2, bf16[1,1024,896]{2,1,0:T(8,128)(2,1)} %all-gather.7.cloned.1.call-done, s32[]{:T(128)S(6)} %select_n.18), kind=kOutput, calls=%fused_computation.59 | convolution fusion | flops 2281177088 | bytes 14843908 | tf_op jit(solution)/shard_map/dot_general | solution.py:270
  415.7 2.1 copy-done.1
  417.8 1.5 constant_dynamic-slice_fusion.2
  419.3 0.5 collective-permute-start.3
  419.8 26.0 %fusion.43 = f32[224,4864]{1,0:T(8,128)} fusion(bf16[1024,4864]{1,0:T(8,128)(2,1)} %convolution_convert_fusion.1, bf16[3,4864,896]{2,1,0:T(8,128)(2,1)} %w2_hbm.1, bf16[1,1024,896]{2,1,0:T(8,128)(2,1)} %all-gather.9.cloned.1.call-done, bf16[1024,896]{1,0:T(8,128)(2,1)} %bitcast.71, s32[]{:T(128)S(6)} %select_n.18), kind=kOutput, calls=%fused_computation.62 | convolution fusion | flops 11271405568 | bytes 25395204 | tf_op jit(solution)/shard_map/dot_general | solution.py:269
  445.8 1.9 constant_dynamic-slice_fusion.4
  447.7 0.0 slice-start.3
  447.8 0.1 collective-permute-start.1
  447.8 11.2 %fusion.35 = f32[4864,224]{0,1:T(8,128)S(1)} fusion(bf16[1024,4864]{1,0:T(8,128)(2,1)} %convolution_convert_fusion.1, bf16[1,1024,896]{2,1,0:T(8,128)(2,1)} %all-gather.9.cloned.1.call-done, s32[]{:T(128)S(6)} %select_n.18), kind=kOutput, calls=%fused_computation.58 | convolution fusion | flops 2281177088 | bytes 14843908 | tf_op jit(solution)/shard_map/dot_general | solution.py:270
  459.1 0.2 constant_dynamic-slice_fusion.1
  459.2 0.0 slice-start.5
  459.2 0.0 slice-start.6
  459.3 0.0 collective-permute-done.2
  459.3 0.5 collective-permute-start.4
  459.8 2.3 add_bitcast_fusion.3
  462.1 0.0 slice-start.7
  462.1 2.7 add_bitcast_fusion
  464.8 1.9 add_bitcast_fusion.5
  466.8 0.2 add_bitcast_fusion.4
  467.0 3.3 pad_maximum_fusion
  470.3 1.9 add_bitcast_fusion.2
  472.2 0.2 add_bitcast_fusion.1
  472.5 3.3 pad_maximum_fusion.1
  (31 shorter events, 0.1 us)
Async XLA Ops:
  7.2 325.4 %all-gather.11.cloned.1.call-start = ((), (), s32[]{:S(2)}) async-start(), calls=%async_computation.2 | async-start | bytes 2293760 | tf_op jit(solution)/shard_map/all_gather | solution.py:257
  237.2 138.4 %all-gather.7.cloned.1.call-start = ((), (), s32[]{:S(2)}) async-start(), calls=%async_computation | async-start | bytes 2293760 | tf_op jit(solution)/shard_map/all_gather | solution.py:257
  238.0 181.8 %all-gather.9.cloned.1.call-start = ((), (), s32[]{:S(2)}) async-start(), calls=%async_computation.1 | async-start | bytes 2293760 | tf_op jit(solution)/shard_map/all_gather | solution.py:257
  282.1 18.2 %copy-start.4 = (bf16[1,4,256,896]{3,2,1,0:T(8,128)(2,1)}, bf16[1,4,256,896]{3,2,1,0:T(8,128)(2,1)S(1)}, u32[]{:S(2)}) copy-start(bf16[1,4,256,896]{3,2,1,0:T(8,128)(2,1)S(1)} %get-tuple-element.10) | copy-start | bytes 5505028
  282.2 18.2 %copy-start.3 = (bf16[1,4,256,896]{3,2,1,0:T(8,128)(2,1)}, bf16[1,4,256,896]{3,2,1,0:T(8,128)(2,1)S(1)}, u32[]{:S(2)}) copy-start(bf16[1,4,256,896]{3,2,1,0:T(8,128)(2,1)S(1)} %get-tuple-element.9) | copy-start | bytes 5505028
  282.2 34.3 %copy-start.2 = (bf16[1,4,256,896]{3,2,1,0:T(8,128)(2,1)}, bf16[1,4,256,896]{3,2,1,0:T(8,128)(2,1)S(1)}, u32[]{:S(2)}) copy-start(bf16[1,4,256,896]{3,2,1,0:T(8,128)(2,1)S(1)} %get-tuple-element.11) | copy-start | bytes 5505028
  343.5 2.1 copy-start
  375.1 84.2 %collective-permute-start.2 = (f32[112,4864]{1,0:T(8,128)}, f32[112,4864]{1,0:T(8,128)}, u32[]{:S(2)}, u32[]{:S(2)}) collective-permute-start(f32[112,4864]{1,0:T(8,128)} %constant_dynamic-slice_fusion.3), channel_id=1, source_target_pairs={{0,1},{1,0},{2,3},{3,2},{4,5},{5,4},{6,7},{7,6},{8,9},{9,8},{10,11... | collective-permute-start | bytes 6537224 | tf_op jit(solution)/shard_map/ppermute | solution.py:275
  375.1 87.0 %collective-permute-start.5 = (f32[4864,112]{0,1:T(8,128)S(1)}, f32[4864,112]{0,1:T(8,128)}, u32[]{:S(2)}, u32[]{:S(2)}) collective-permute-start(f32[4864,112]{0,1:T(8,128)S(1)} %constant_dynamic-slice_fusion), channel_id=1, source_target_pairs={{0,1},{1,0},{2,3},{3,2},{4,5},{5,4},{6,7},{7,6},{8,9},{9,8},{10,11... | collective-permute-start | bytes 6537224 | tf_op jit(solution)/shard_map/ppermute | solution.py:276
  404.7 60.1 %collective-permute-start = (f32[112,4864]{1,0:T(8,128)}, f32[112,4864]{1,0:T(8,128)}, u32[]{:S(2)}, u32[]{:S(2)}) collective-permute-start(f32[112,4864]{1,0:T(8,128)} %constant_dynamic-slice_fusion.5), channel_id=1, source_target_pairs={{0,1},{1,0},{2,3},{3,2},{4,5},{5,4},{6,7},{7,6},{8,9},{9,8},{10,11... | collective-permute-start | bytes 6537224 | tf_op jit(solution)/shard_map/ppermute | solution.py:275
  415.7 2.1 copy-start.1
  419.3 51.0 %collective-permute-start.3 = (f32[4864,112]{0,1:T(8,128)}, f32[4864,112]{0,1:T(8,128)}, u32[]{:S(2)}, u32[]{:S(2)}) collective-permute-start(f32[4864,112]{0,1:T(8,128)} %constant_dynamic-slice_fusion.2), channel_id=1, source_target_pairs={{0,1},{1,0},{2,3},{3,2},{4,5},{5,4},{6,7},{7,6},{8,9},{9,8},{10,11... | collective-permute-start | bytes 6537224 | tf_op jit(solution)/shard_map/ppermute | solution.py:276
  445.8 14.0 %slice-start.2 = ((s8[4358144]{0:T(1024)(128)(4,1)}), s8[4194304]{0:T(1024)(128)(4,1)S(1)}, s32[]{:S(2)}) async-start(s8[4358144]{0:T(1024)(128)(4,1)} %bitcast.64), calls=%async_computation.5 | async-start | bytes 8388608
  447.7 12.1 %slice-start.3 = ((s8[4358144]{0:T(1024)(128)(4,1)}), s8[163840]{0:T(1024)(128)(4,1)S(1)}, s32[]{:S(2)}) async-start(s8[4358144]{0:T(1024)(128)(4,1)} %bitcast.64), calls=%async_computation.6 | async-start | bytes 327680
  447.8 19.0 %collective-permute-start.1 = (f32[112,4864]{1,0:T(8,128)S(1)}, f32[112,4864]{1,0:T(8,128)S(1)}, u32[]{:S(2)}, u32[]{:S(2)}) collective-permute-start(f32[112,4864]{1,0:T(8,128)S(1)} %constant_dynamic-slice_fusion.4), channel_id=1, source_target_pairs={{0,1},{1,0},{2,3},{3,2},{4,5},{5,4},{6,7},{7,6},{8,9},{9,8},{10,11... | collective-permute-start | bytes 6537224 | tf_op jit(solution)/shard_map/ppermute | solution.py:275
  459.1 5.7 %slice-start.4 = ((s8[4358144]{0:T(1024)(128)(4,1)}), s8[4194304]{0:T(1024)(128)(4,1)S(1)}, s32[]{:S(2)}) async-start(s8[4358144]{0:T(1024)(128)(4,1)} %bitcast.66), calls=%async_computation.7 | async-start | bytes 8388608
  459.2 5.5 %slice-start.5 = ((s8[4358144]{0:T(1024)(128)(4,1)}), s8[163840]{0:T(1024)(128)(4,1)S(1)}, s32[]{:S(2)}) async-start(s8[4358144]{0:T(1024)(128)(4,1)} %bitcast.66), calls=%async_computation.8 | async-start | bytes 327680
  459.2 7.5 %slice-start.6 = ((s8[4358144]{0:T(1024)(128)(4,1)}), s8[163840]{0:T(1024)(128)(4,1)S(1)}, s32[]{:S(2)}) async-start(s8[4358144]{0:T(1024)(128)(4,1)} %bitcast.68), calls=%async_computation.9 | async-start | bytes 327680
  459.3 12.9 %collective-permute-start.4 = (f32[4864,112]{0,1:T(8,128)S(1)}, f32[4864,112]{0,1:T(8,128)S(1)}, u32[]{:S(2)}, u32[]{:S(2)}) collective-permute-start(f32[4864,112]{0,1:T(8,128)S(1)} %constant_dynamic-slice_fusion.1), channel_id=1, source_target_pairs={{0,1},{1,0},{2,3},{3,2},{4,5},{5,4},{6,7},{7,6},{8,9},{9,8},{10,11... | collective-permute-start | bytes 6537224 | tf_op jit(solution)/shard_map/ppermute | solution.py:276
  462.1 4.7 slice-start.7
  466.7 3.6 slice-start
  467.0 3.3 slice-start.1
Sparse Core Ops, SparseCore 0:
  237.3 31.0 all-gather.10
  270.3 32.7 all-gather.6
  304.9 32.7 all-gather.8

commit v3 on v2

v3 whole, which is shorter than its diff:
```python
import functools

import jax
import jax.numpy as jnp
from jax import lax
from jax.experimental import pallas as pl
from jax.experimental.pallas import tpu as pltpu
from jax.sharding import PartitionSpec as P

CONTRACT_LAST = (((1,), (1,)), ((), ()))
MESH = pl.DeviceIdType.MESH
GELU_C = 0.7978845608028654
GELU_A = 0.044715
CHIPS = 4


def gelu_wide(u):
    th = jnp.tanh(u * (GELU_C + (GELU_C * GELU_A) * (u * u)))
    return u * (0.5 + 0.5 * th)


def gelu_slope(u):
    sq = u * u
    th = jnp.tanh(u * (GELU_C + (GELU_C * GELU_A) * sq))
    half = 0.5 + 0.5 * th
    return half + (0.5 * u) * (1.0 - th * th) * (GELU_C + (3.0 * GELU_C * GELU_A) * sq)


def chain_kernel(stages, total_tokens, x_ref, y_ref, w1_hbm, w2_hbm, h_all, e_out, e_top, loss_ref,
                 w1, w2, ut, g_buf, hs, e_t, e_nat, y_buf, loss_buf, loss_tot,
                 w1_sem, w2_sem, io_sem, hop_send, hop_recv, ag_send, ag_recv, ls_send, ls_recv):
    stage = lax.axis_index('stage')
    data = lax.axis_index('data')
    chip = data // 2
    core = data % 2
    n_layers, width, ffn = w1.shape
    not_first = stage > 0
    not_last = stage < stages - 1

    def load_w1(l):
        return pltpu.make_async_copy(w1_hbm.at[l], w1.at[l], w1_sem.at[l])

    def load_w2(l, s):
        return pltpu.make_async_copy(w2_hbm.at[l], w2.at[l % 2], w2_sem.at[s])

    x_copy = pltpu.make_async_copy(x_ref, hs.at[0], io_sem.at[0])
    y_copy = pltpu.make_async_copy(y_ref, y_buf, io_sem.at[1])

    @pl.when(jnp.logical_not(not_first))
    def _():
        x_copy.start()

    load_w1(0).start()
    load_w2(0, 0).start()
    load_w1(1).start()
    load_w2(1, 1).start()
    load_w1(2).start()

    @pl.when(jnp.logical_not(not_last))
    def _():
        y_copy.start()

    peers = []
    for j in range(1, CHIPS):
        px = (chip // 2 + j // 2) % 2
        py = (chip % 2 + j % 2) % 2
        peers.append((px * 2 + py) * 2 + core)

    barrier = pltpu.get_barrier_semaphore()
    for k in range(1, 2 * CHIPS):
        pl.semaphore_signal(barrier, inc=1, device_id=(stage, (data + k) % (2 * CHIPS)), device_id_type=MESH)

    @pl.when(not_first)
    def _():
        pl.semaphore_signal(barrier, inc=1, device_id=(stage - 1, data), device_id_type=MESH)

    @pl.when(not_last)
    def _():
        pl.semaphore_signal(barrier, inc=1, device_id=(stage + 1, data), device_id_type=MESH)

    pl.semaphore_wait(barrier, 2 * CHIPS - 1 + jnp.minimum(stage, 1) + jnp.minimum(stages - 1 - stage, 1))

    def hop_up():
        return pltpu.make_async_remote_copy(
            src_ref=hs.at[n_layers], dst_ref=hs.at[0], send_sem=hop_send.at[0], recv_sem=hop_recv.at[0],
            device_id=(stage + 1, data), device_id_type=MESH)

    def hop_down():
        return pltpu.make_async_remote_copy(
            src_ref=e_t.at[0], dst_ref=e_t.at[n_layers], send_sem=hop_send.at[1], recv_sem=hop_recv.at[1],
            device_id=(stage - 1, data), device_id_type=MESH)

    def gather(l, j):
        return pltpu.make_async_remote_copy(
            src_ref=hs.at[l], dst_ref=h_all.at[l, chip], send_sem=ag_send.at[l, j], recv_sem=ag_recv.at[l, j],
            device_id=(stage, peers[j]), device_id_type=MESH)

    def keep(l):
        return pltpu.make_async_copy(hs.at[l], h_all.at[l, chip], io_sem.at[2 + l])

    top = n_layers - 1

    def gather_top(j):
        return pltpu.make_async_remote_copy(
            src_ref=e_nat.at[top], dst_ref=e_top.at[chip], send_sem=ag_send.at[n_layers, j],
            recv_sem=ag_recv.at[n_layers, j], device_id=(stage, peers[j]), device_id_type=MESH)

    def keep_e(l):
        dst = e_top.at[chip] if l == top else e_out.at[l]
        return pltpu.make_async_copy(e_nat.at[l], dst, io_sem.at[5 + l])

    def share_loss(k):
        return pltpu.make_async_remote_copy(
            src_ref=loss_buf.at[data], dst_ref=loss_buf.at[data], send_sem=ls_send.at[k - 1], recv_sem=ls_recv.at[k - 1],
            device_id=(stage, (data + k) % (2 * CHIPS)), device_id_type=MESH)

    def loss_down():
        return pltpu.make_async_remote_copy(
            src_ref=loss_tot, dst_ref=loss_tot, send_sem=hop_send.at[2], recv_sem=hop_recv.at[2],
            device_id=(stage - 1, data), device_id_type=MESH)

    @pl.when(not_first)
    def _():
        hop_up().wait_recv()

    @pl.when(jnp.logical_not(not_first))
    def _():
        x_copy.wait()

    def fwd_layer(l, carry):
        for j in range(CHIPS - 1):
            gather(l, j).start()
        keep(l).start()
        load_w1(l).wait()
        h = hs[l]
        for c in range(ffn // 256):
            cols = slice(c * 256, (c + 1) * 256)
            u = jnp.dot(h, w1[l, :, cols], preferred_element_type=jnp.float32).astype(jnp.bfloat16)
            ut[l, cols, :] = u.T
            g_buf[:, cols] = gelu_wide(u.astype(jnp.float32)).astype(jnp.bfloat16)
        load_w2(l, l).wait()
        branch = jnp.dot(g_buf[...], w2[l % 2], preferred_element_type=jnp.float32)
        hs[l + 1] = (h.astype(jnp.float32) + branch).astype(jnp.bfloat16)

        @pl.when(l == 0)
        def _():
            load_w2(2, 2).start()
        return carry

    lax.fori_loop(0, n_layers, fwd_layer, 0)

    @pl.when(not_last)
    def _():
        hop_up().start()
        hop_up().wait_send()
        hop_down().wait_recv()

    @pl.when(jnp.logical_not(not_last))
    def _():
        y_copy.wait()
        diff = hs[n_layers].astype(jnp.float32) - y_buf[...].astype(jnp.float32)
        e_t[n_layers] = (diff / total_tokens).T.astype(jnp.bfloat16)
        loss_buf[data] = jnp.full((8, 128), jnp.sum(diff * diff), jnp.float32)
        for k in range(1, 2 * CHIPS):
            share_loss(k).start()

    rows_c = ffn // 4

    def bwd_layer(i, carry):
        l = n_layers - 1 - i

        @pl.when(l == 0)
        def _():
            load_w2(0, 3).wait()
        e_cur = e_t[l + 1]
        e_nat[l] = e_cur.T
        for c in range(4):
            rows = slice(c * rows_c, (c + 1) * rows_c)
            dg = jnp.dot(w2[l % 2, rows, :], e_cur, preferred_element_type=jnp.float32).astype(jnp.bfloat16)
            slope = gelu_slope(ut[l, rows, :].astype(jnp.float32))
            ut[l, rows, :] = (dg.astype(jnp.float32) * slope).astype(jnp.bfloat16)

        @pl.when(l == 2)
        def _():
            load_w2(0, 3).start()
            for j in range(CHIPS - 1):
                gather_top(j).start()
            keep_e(top).start()

        @pl.when(jnp.logical_or(not_first, l > 0))
        def _():
            back = jnp.dot(w1[l], ut[l], preferred_element_type=jnp.float32)
            e_t[l] = (e_cur.astype(jnp.float32) + back).astype(jnp.bfloat16)
        return carry

    lax.fori_loop(0, n_layers, bwd_layer, 0)

    @pl.when(not_first)
    def _():
        hop_down().start()

    for l in range(top):
        keep_e(l).start()

    @pl.when(not_last)
    def _():
        loss_down().wait_recv()

    @pl.when(jnp.logical_not(not_last))
    def _():
        for k in range(1, 2 * CHIPS):
            share_loss(k).wait_send()
            share_loss(k).wait_recv()
        total = loss_buf[0]
        for k in range(1, 2 * CHIPS):
            total = total + loss_buf[k]
        loss_tot[...] = total / (2 * total_tokens)

    loss_ref[...] = loss_tot[...]

    @pl.when(not_first)
    def _():
        loss_down().start()

    for l in range(n_layers):
        keep_e(l).wait()
        keep(l).wait()
        for j in range(CHIPS - 1):
            gather(l, j).wait_send()
            gather(l, j).wait_recv()
    for j in range(CHIPS - 1):
        gather_top(j).wait_send()
        gather_top(j).wait_recv()

    @pl.when(not_first)
    def _():
        hop_down().wait_send()
        loss_down().wait_send()


def run_chain(x_rows, y_rows, w_up, w_down, stages, total_tokens):
    rows, width = x_rows.shape
    n_layers, _, ffn = w_up.shape
    bf = jnp.bfloat16
    any_spec = pl.BlockSpec(memory_space=pl.ANY)
    return pl.pallas_call(
        functools.partial(chain_kernel, stages, total_tokens),
        out_shape=(
            jax.ShapeDtypeStruct((n_layers, CHIPS, rows, width), bf),
            jax.ShapeDtypeStruct((n_layers - 1, rows, width), bf),
            jax.ShapeDtypeStruct((CHIPS, rows, width), bf),
            jax.ShapeDtypeStruct((8, 128), jnp.float32),
        ),
        in_specs=[any_spec] * 4,
        out_specs=(any_spec, any_spec, any_spec, pl.BlockSpec(memory_space=pltpu.VMEM)),
        scratch_shapes=[
            pltpu.VMEM((n_layers, width, ffn), bf),
            pltpu.VMEM((2, ffn, width), bf),
            pltpu.VMEM((n_layers, ffn, rows), bf),
            pltpu.VMEM((rows, ffn), bf),
            pltpu.VMEM((n_layers + 1, rows, width), bf),
            pltpu.VMEM((n_layers + 1, width, rows), bf),
            pltpu.VMEM((n_layers, rows, width), bf),
            pltpu.VMEM((rows, width), bf),
            pltpu.VMEM((2 * CHIPS, 8, 128), jnp.float32),
            pltpu.VMEM((8, 128), jnp.float32),
            pltpu.SemaphoreType.DMA((3,)),
            pltpu.SemaphoreType.DMA((4,)),
            pltpu.SemaphoreType.DMA((8,)),
            pltpu.SemaphoreType.DMA((3,)),
            pltpu.SemaphoreType.DMA((3,)),
            pltpu.SemaphoreType.DMA((4, 3)),
            pltpu.SemaphoreType.DMA((4, 3)),
            pltpu.SemaphoreType.DMA((7,)),
            pltpu.SemaphoreType.DMA((7,)),
        ],
        compiler_params=pltpu.CompilerParams(collective_id=0, has_side_effects=True, vmem_limit_bytes=67043328),
    )(x_rows, y_rows, w_up, w_down)


CHUNK = 256
RING = 4


def weight_kernel(h_hbm, e_own, e_top, w1_hbm, w2_hbm, out1, out2,
                  h_buf, e_buf, w1s, w2s, hct, ect, u_a, dg_a, u_b, dg_b, part, recv, turn,
                  w_sem, h_sem, e_sem, o_sem, ag_send, ag_recv, x_send, x_recv):
    stage = lax.axis_index('stage')
    data = lax.axis_index('data')
    chip = data // 2
    core = data % 2
    n_layers, width, ffn = w1_hbm.shape
    n_chunks = ffn // CHUNK
    total = n_layers * n_chunks
    blk = out1.shape[1]
    rows = e_own.shape[1]
    top = n_layers - 1
    partner = data + 1 - 2 * core

    def load_w(q):
        qq = jnp.minimum(q, total - 1)
        l = top - qq // n_chunks
        cols = pl.ds(pl.multiple_of((qq % n_chunks) * CHUNK, CHUNK), CHUNK)
        s = q % RING
        return (pltpu.make_async_copy(w1_hbm.at[l, :, cols], w1s.at[s], w_sem.at[0, s]),
                pltpu.make_async_copy(w2_hbm.at[l, cols, :], w2s.at[s], w_sem.at[1, s]))

    def load_h(l):
        return pltpu.make_async_copy(h_hbm.at[l], h_buf.at[l], h_sem.at[l])

    load_h(top).start()
    top_copy = pltpu.make_async_copy(e_top, e_buf.at[top], e_sem.at[top])
    top_copy.start()
    for q in range(RING - 1):
        for cp in load_w(q):
            cp.start()

    peers = []
    for j in range(1, CHIPS):
        px = (chip // 2 + j // 2) % 2
        py = (chip % 2 + j % 2) % 2
        peers.append((px * 2 + py) * 2 + core)
    barrier = pltpu.get_barrier_semaphore()
    for p in peers + [partner]:
        pl.semaphore_signal(barrier, inc=1, device_id=(stage, p), device_id_type=MESH)
    pl.semaphore_wait(barrier, CHIPS)

    def gather(l, j):
        return pltpu.make_async_remote_copy(
            src_ref=e_own.at[l], dst_ref=e_buf.at[l, chip], send_sem=ag_send.at[l, j], recv_sem=ag_recv.at[l, j],
            device_id=(stage, peers[j]), device_id_type=MESH)

    def keep(l):
        return pltpu.make_async_copy(e_own.at[l], e_buf.at[l, chip], e_sem.at[l])

    for l in reversed(range(top)):
        for j in range(CHIPS - 1):
            gather(l, j).start()
        keep(l).start()
        load_h(l).start()

    def swap(l, par, k):
        return pltpu.make_async_remote_copy(
            src_ref=part.at[par, k, 1 - core], dst_ref=recv.at[l, k], send_sem=x_send.at[l, k], recv_sem=x_recv.at[l, k],
            device_id=(stage, partner), device_id_type=MESH)

    def put_one(l, par):
        return pltpu.make_async_copy(part.at[par, 0, core], out1.at[l], o_sem.at[0])

    def put_two(l):
        return pltpu.make_async_copy(turn, out2.at[l], o_sem.at[1])

    def finish(l, par):
        for k in range(2):
            swap(l, par, k).wait_send()
            swap(l, par, k).wait_recv()

        def add(c, carry):
            cols = pl.ds(pl.multiple_of(c * CHUNK, CHUNK), CHUNK)
            part[par, 0, core, :, cols] = part[par, 0, core, :, cols] + recv[l, 0, :, cols]
            both = part[par, 1, core, :, cols] + recv[l, 1, :, cols]
            turn[cols, :] = both.T
            return carry

        lax.fori_loop(0, n_chunks, add, 0)
        put_one(l, par).start()
        put_two(l).start()
        put_one(l, par).wait()
        put_two(l).wait()

    def layer_step(li, carry):
        l = top - li
        par = li % 2
        load_h(l).wait()

        @pl.when(li == 0)
        def _():
            top_copy.wait()

        @pl.when(li > 0)
        def _():
            keep(l).wait()
            for j in range(CHIPS - 1):
                gather(l, j).wait_recv()

        n_rows = CHIPS * rows
        for k in range(CHIPS):
            @pl.when(chip == k)
            def _():
                lanes = slice(k * 2 * blk, (k + 1) * 2 * blk)
                for r in range(CHIPS):
                    hct[:, r * rows:(r + 1) * rows] = h_buf[l, r, :, lanes].T
                    ect[:, r * rows:(r + 1) * rows] = e_buf[l, r, :, lanes].T

        def mm(c, u_ref, dg_ref):
            q = li * n_chunks + c
            for cp in load_w(q):
                cp.wait()
            for cp in load_w(q + RING - 1):
                cp.start()
            s = q % RING
            h = h_buf[l].reshape(n_rows, width)
            e = e_buf[l].reshape(n_rows, width)
            u_ref[...] = jnp.dot(h, w1s[s], preferred_element_type=jnp.float32).astype(jnp.bfloat16)
            dg_ref[...] = lax.dot_general(e, w2s[s], CONTRACT_LAST, preferred_element_type=jnp.float32).astype(jnp.bfloat16)

        def ew(c, u_ref, dg_ref):
            cols = pl.ds(pl.multiple_of(c * CHUNK, CHUNK), CHUNK)
            u = u_ref[...].astype(jnp.float32)
            sq = u * u
            half = 0.5 + 0.5 * jnp.tanh(u * (GELU_C + (GELU_C * GELU_A) * sq))
            g = (u * half).astype(jnp.bfloat16)
            slope = half + (half - half * half) * (u * (2.0 * GELU_C + (6.0 * GELU_C * GELU_A) * sq))
            du = (dg_ref[...].astype(jnp.float32) * slope).astype(jnp.bfloat16)
            d1 = jnp.dot(hct[...], du, preferred_element_type=jnp.float32)
            d2 = jnp.dot(ect[...], g, preferred_element_type=jnp.float32)
            for k in range(2):
                part[par, 0, k, :, cols] = d1[k * blk:(k + 1) * blk]
                part[par, 1, k, :, cols] = d2[k * blk:(k + 1) * blk]

        mm(0, u_a, dg_a)

        def pair(i, c2):
            mm(2 * i + 1, u_b, dg_b)
            ew(2 * i, u_a, dg_a)
            mm(2 * i + 2, u_a, dg_a)
            ew(2 * i + 1, u_b, dg_b)
            return c2

        lax.fori_loop(0, n_chunks // 2, pair, 0)
        ew(n_chunks - 1, u_a, dg_a)
        for k in range(2):
            swap(l, par, k).start()

        @pl.when(li > 0)
        def _():
            finish(l + 1, (li + 1) % 2)
        return carry

    lax.fori_loop(0, n_layers, layer_step, 0)
    finish(0, top % 2)
    for q in range(total, total + RING - 1):
        for cp in load_w(q):
            cp.wait()
    for l in range(top):
        for j in range(CHIPS - 1):
            gather(l, j).wait_send()


def run_weights(h_gath, e_own, e_top, w_up, w_down):
    n_layers, _, rows, width = h_gath.shape
    ffn = w_up.shape[2]
    blk = width // (2 * CHIPS)
    bf, f32 = jnp.bfloat16, jnp.float32
    any_spec = pl.BlockSpec(memory_space=pl.ANY)
    dma = pltpu.SemaphoreType.DMA
    return pl.pallas_call(
        weight_kernel,
        out_shape=(
            jax.ShapeDtypeStruct((n_layers, blk, ffn), f32),
            jax.ShapeDtypeStruct((n_layers, ffn, blk), f32),
        ),
        in_specs=[any_spec] * 5,
        out_specs=(any_spec, any_spec),
        scratch_shapes=[
            pltpu.VMEM((n_layers, CHIPS, rows, width), bf),
            pltpu.VMEM((n_layers, CHIPS, rows, width), bf),
            pltpu.VMEM((RING, width, CHUNK), bf),
            pltpu.VMEM((RING, CHUNK, width), bf),
            pltpu.VMEM((2 * blk, CHIPS * rows), bf),
            pltpu.VMEM((2 * blk, CHIPS * rows), bf),
            pltpu.VMEM((CHIPS * rows, CHUNK), bf),
            pltpu.VMEM((CHIPS * rows, CHUNK), bf),
            pltpu.VMEM((CHIPS * rows, CHUNK), bf),
            pltpu.VMEM((CHIPS * rows, CHUNK), bf),
            pltpu.VMEM((2, 2, 2, blk, ffn), f32),
            pltpu.VMEM((n_layers, 2, blk, ffn), f32),
            pltpu.VMEM((ffn, blk), f32),
            dma((2, RING)), dma((3,)), dma((3,)), dma((2,)),
            dma((2, 3)), dma((2, 3)), dma((3, 2)), dma((3, 2)),
        ],
        compiler_params=pltpu.CompilerParams(collective_id=1, has_side_effects=True, vmem_limit_bytes=67043328),
    )(h_gath, e_own, e_top, w_up, w_down)


def solution(mesh):
    stages = mesh.shape['stage']
    replicas = mesh.shape['data']

    def per_device(x_loc, y_loc, w_up, w_down):
        n_micro, n_tokens, n_width = x_loc.shape
        n_layers = w_up.shape[0]
        rows = n_micro * n_tokens
        total_tokens = replicas * rows
        x_rows = x_loc.reshape(rows, n_width)
        y_rows = y_loc.reshape(rows, n_width)
        h_gath, e_own, e_top, loss = run_chain(x_rows, y_rows, w_up, w_down, stages, total_tokens)
        grad_up, grad_down = run_weights(h_gath, e_own, e_top, w_up, w_down)
        return loss[0, 0], grad_up, grad_down

    return jax.shard_map(
        per_device,
        mesh=mesh,
        in_specs=(P('data', None, None), P('data', None, None), P('stage', None, None), P('stage', None, None)),
        out_specs=(P(), P('stage', 'data', None), P('stage', None, 'data')),
        check_vma=False,
    )
```

time: 488 us -> 372 us (0.76)
  matrix products: 162 us -> 0 us
  Pallas kernels: 228 us -> 355 us
  blocking collectives: 38.3 us -> 0 us
  other arithmetic: 17.1 us -> 0 us
  between operations: 15 us -> 0.65 us
    dot_general x9 -> x0, matrix products: 162 us -> none  [the longest x3 78.3 us: per_device(): lax.dot_general(h_cols, du, CONTRACT_FIRST, preferred_element_type=jnp.fl...]
    pallas_call x0 -> x1, Pallas kernels: none -> 124 us  [run_weights(): pl.pallas_call(weight_kernel, out_shape=(jax.ShapeDtypeStruct((n_layers,...]
    psum x1 -> x0, blocking collectives: 38.3 us -> none  [per_device(): lax.psum(jnp.sum(loss_part) / (2 * total_tokens), ('stage', 'data'))]
    another operation x8 -> x0, other arithmetic: 15.8 us -> none  [per_device(): return (total_loss, jnp.stack(up_out), jnp.stack(down_out))]
    unnamed x26 -> x2, local copies, waits for them, and re-layouts: 4.26 us -> 14.4 us
    dynamic_slice x6 -> x0, local copies, waits for them, and re-layouts: 9.89 us -> none  [the longest x3 8.08 us: per_device(): lax.dynamic_slice_in_dim(g_one, (1 - core) * width_blk, width_blk, 0)]
  transfers between devices with their start and end apart: 9 -> 0, of which waited for: 0 -> 0; matrix products, arithmetic and copies ran while one was open for 39% -> 0% of each run, Pallas kernels for 0% -> 0%
where the time goes in v3:
time: 372 us; the launch traced here: 371 us
  Pallas kernels  355 us (95%)
  local copies, waits for them, and re-layouts  15.6 us (4%)
    pallas_call x1, Pallas kernels, run_chain(): pl.pallas_call(functools.partial(chain_kernel, stages, total_tokens), out...  230 us
    pallas_call x1, Pallas kernels, run_weights(): pl.pallas_call(weight_kernel, out_shape=(jax.ShapeDtypeStruct((n_layers,...  124 us
    unnamed x2, local copies, waits for them, and re-layouts  14.4 us

profile of v3, /device:TPU:0, one launch (start us, length us, event | category | flops | bytes accessed | tf_op | source)
XLA Modules:
  0.0 371.1 jit_solution(10304496177779266618)
XLA Ops:
  0.6 230.5 %shard_map.67 = (bf16[3,4,256,896]{3,2,1,0:T(8,128)(2,1)}, bf16[2,256,896]{2,1,0:T(8,128)(2,1)}, bf16[4,256,896]{2,1,0:T(8,128)(2,1)}, f32[8,128]{1,0:T(8,128)}) custom-call(bf16[256,896]{1,0:T(8,128)(2,1)} %bitcast.3, bf16[256,896]{1,0:T(8,128)(2,1)} %bitcast.4, bf16[3,896,4864]{2,1,0:T(8,128)(2,1)} %w1_hbm.3, bf16[3,4864,896]{2,1,0:T(8,128)(2,1)} %w2_hbm.3), custom_call_target="tpu_custom_call" | custom-call | tf_op jit(solution)/shard_map/pallas_call | solution.py:246
  231.1 1.2 slice.3
  232.3 124.4 %shard_map.68 = (f32[3,112,4864]{2,1,0:T(8,128)}, f32[3,4864,112]{2,1,0:T(8,128)}) custom-call(bf16[3,4,256,896]{3,2,1,0:T(8,128)(2,1)} %get-tuple-element.10.h_hbm, bf16[2,256,896]{2,1,0:T(8,128)(2,1)} %get-tuple-element.11.e_own, bf16[4,256,896]{2,1,0:T(8,128)(2,1)} %get-tuple-element.12.e_top, bf16[3,896,4864]{2,1,0:T(8,128)(2,1)} %w1_hbm.3, ...), custom_call_target="tpu_custom_call" | custom-call | tf_op jit(solution)/shard_map/pallas_call | solution.py:457
  356.7 8.4 %copy.7 = f32[3,4864,112]{1,2,0:T(8,128)} copy(f32[3,4864,112]{2,1,0:T(8,128)} %get-tuple-element.17) | data formatting | bytes 13074432
  365.1 6.1 %copy.9 = f32[3,112,4864]{2,1,0:T(8,128)} copy(f32[3,112,4864]{2,1,0:T(8,128)} %get-tuple-element.22) | data formatting | bytes 13074432

commit v4 on v3

--- a/solution.py
+++ b/solution.py
@@ -28,7 +28,7 @@
 
 def chain_kernel(stages, total_tokens, x_ref, y_ref, w1_hbm, w2_hbm, h_all, e_out, e_top, loss_ref,
                  w1, w2, ut, g_buf, hs, e_t, e_nat, y_buf, loss_buf, loss_tot,
-                 w1_sem, w2_sem, io_sem, hop_send, hop_recv, ag_send, ag_recv, ls_send, ls_recv):
+                 w1_sem, w2_sem, io_sem, hop_send, hop_recv, ag_send, ag_recv, ls_send, ls_recv, turn_sem):
     stage = lax.axis_index('stage')
     data = lax.axis_index('data')
     chip = data // 2
@@ -36,6 +36,9 @@
     n_layers, width, ffn = w1.shape
     not_first = stage > 0
     not_last = stage < stages - 1
+    is_first = jnp.logical_not(not_first)
+    is_last = jnp.logical_not(not_last)
+    pieces = ((0, 512), (512, width))
 
     def load_w1(l):
         return pltpu.make_async_copy(w1_hbm.at[l], w1.at[l], w1_sem.at[l])
@@ -51,10 +54,13 @@
         x_copy.start()
 
     load_w1(0).start()
-    load_w2(0, 0).start()
-    load_w1(1).start()
-    load_w2(1, 1).start()
-    load_w1(2).start()
+
+    @pl.when(not_first)
+    def _():
+        load_w2(0, 0).start()
+        load_w1(1).start()
+        load_w2(1, 1).start()
+        load_w1(2).start()
 
     @pl.when(jnp.logical_not(not_last))
     def _():
@@ -80,15 +86,17 @@
 
     pl.semaphore_wait(barrier, 2 * CHIPS - 1 + jnp.minimum(stage, 1) + jnp.minimum(stages - 1 - stage, 1))
 
-    def hop_up():
-        return pltpu.make_async_remote_copy(
-            src_ref=hs.at[n_layers], dst_ref=hs.at[0], send_sem=hop_send.at[0], recv_sem=hop_recv.at[0],
-            device_id=(stage + 1, data), device_id_type=MESH)
-
-    def hop_down():
-        return pltpu.make_async_remote_copy(
-            src_ref=e_t.at[0], dst_ref=e_t.at[n_layers], send_sem=hop_send.at[1], recv_sem=hop_recv.at[1],
-            device_id=(stage - 1, data), device_id_type=MESH)
+    def hop_up(p):
+        lanes = slice(*pieces[p])
+        return pltpu.make_async_remote_copy(
+            src_ref=hs.at[n_layers, :, lanes], dst_ref=hs.at[0, :, lanes], send_sem=hop_send.at[0, p],
+            recv_sem=hop_recv.at[0, p], device_id=(stage + 1, data), device_id_type=MESH)
+
+    def hop_down(p):
+        subl = slice(*pieces[p])
+        return pltpu.make_async_remote_copy(
+            src_ref=e_t.at[0, subl, :], dst_ref=e_t.at[n_layers, subl, :], send_sem=hop_send.at[1, p],
+            recv_sem=hop_recv.at[1, p], device_id=(stage - 1, data), device_id_type=MESH)
 
     def gather(l, j):
         return pltpu.make_async_remote_copy(
@@ -116,22 +124,31 @@
 
     def loss_down():
         return pltpu.make_async_remote_copy(
-            src_ref=loss_tot, dst_ref=loss_tot, send_sem=hop_send.at[2], recv_sem=hop_recv.at[2],
+            src_ref=loss_tot, dst_ref=loss_tot, send_sem=hop_send.at[2, 0], recv_sem=hop_recv.at[2, 0],
             device_id=(stage - 1, data), device_id_type=MESH)
 
     @pl.when(not_first)
     def _():
-        hop_up().wait_recv()
-
-    @pl.when(jnp.logical_not(not_first))
+        hop_up(0).wait_recv()
+        hop_up(1).wait_recv()
+
+    @pl.when(is_first)
     def _():
         x_copy.wait()
+
+    send_now = jnp.logical_and(not_last, jnp.logical_or(not_first, core == 0))
 
     def fwd_layer(l, carry):
         for j in range(CHIPS - 1):
             gather(l, j).start()
         keep(l).start()
         load_w1(l).wait()
+
+        @pl.when(is_first)
+        def _():
+            @pl.when(l < top)
+            def _():
+                load_w2(l, l).start()
         h = hs[l]
         for c in range(ffn // 256):
             cols = slice(c * 256, (c + 1) * 256)
@@ -139,8 +156,20 @@
             ut[l, cols, :] = u.T
             g_buf[:, cols] = gelu_wide(u.astype(jnp.float32)).astype(jnp.bfloat16)
         load_w2(l, l).wait()
-        branch = jnp.dot(g_buf[...], w2[l % 2], preferred_element_type=jnp.float32)
-        hs[l + 1] = (h.astype(jnp.float32) + branch).astype(jnp.bfloat16)
+
+        @pl.when(is_first)
+        def _():
+            @pl.when(l < top)
+            def _():
+                load_w1(l + 1).start()
+        for p in range(2):
+            lanes = slice(*pieces[p])
+            branch = jnp.dot(g_buf[...], w2[l % 2, :, lanes], preferred_element_type=jnp.float32)
+            hs[l + 1, :, lanes] = (hs[l, :, lanes].astype(jnp.float32) + branch).astype(jnp.bfloat16)
+
+            @pl.when(jnp.logical_and(l == top, send_now))
+            def _():
+                hop_up(p).start()
 
         @pl.when(l == 0)
         def _():
@@ -149,13 +178,27 @@
 
     lax.fori_loop(0, n_layers, fwd_layer, 0)
 
+    @pl.when(jnp.logical_and(is_first, core == 1))
+    def _():
+        pl.semaphore_wait(turn_sem, 1)
+        hop_up(0).start()
+        hop_up(1).start()
+
     @pl.when(not_last)
     def _():
-        hop_up().start()
-        hop_up().wait_send()
-        hop_down().wait_recv()
-
-    @pl.when(jnp.logical_not(not_last))
+        hop_up(0).wait_send()
+        hop_up(1).wait_send()
+
+    @pl.when(jnp.logical_and(is_first, core == 0))
+    def _():
+        pl.semaphore_signal(turn_sem, inc=1, device_id=(stage, data + 1), device_id_type=MESH)
+
+    @pl.when(not_last)
+    def _():
+        hop_down(0).wait_recv()
+        hop_down(1).wait_recv()
+
+    @pl.when(is_last)
     def _():
         y_copy.wait()
         diff = hs[n_layers].astype(jnp.float32) - y_buf[...].astype(jnp.float32)
@@ -164,7 +207,11 @@
         for k in range(1, 2 * CHIPS):
             share_loss(k).start()
 
-    rows_c = ffn // 4
+    e_nat[top] = e_t[n_layers].T
+    for j in range(CHIPS - 1):
+        gather_top(j).start()
+    keep_e(top).start()
+    rows_c = ffn // 19
 
     def bwd_layer(i, carry):
         l = n_layers - 1 - i
@@ -173,8 +220,11 @@
         def _():
             load_w2(0, 3).wait()
         e_cur = e_t[l + 1]
-        e_nat[l] = e_cur.T
-        for c in range(4):
+
+        @pl.when(l < top)
+        def _():
+            e_nat[l] = e_t[l + 1].T
+        for c in range(19):
             rows = slice(c * rows_c, (c + 1) * rows_c)
             dg = jnp.dot(w2[l % 2, rows, :], e_cur, preferred_element_type=jnp.float32).astype(jnp.bfloat16)
             slope = gelu_slope(ut[l, rows, :].astype(jnp.float32))
@@ -183,21 +233,20 @@
         @pl.when(l == 2)
         def _():
             load_w2(0, 3).start()
-            for j in range(CHIPS - 1):
-                gather_top(j).start()
-            keep_e(top).start()
 
         @pl.when(jnp.logical_or(not_first, l > 0))
         def _():
-            back = jnp.dot(w1[l], ut[l], preferred_element_type=jnp.float32)
-            e_t[l] = (e_cur.astype(jnp.float32) + back).astype(jnp.bfloat16)
+            for p in range(2):
+                subl = slice(*pieces[p])
+                back = jnp.dot(w1[l, subl, :], ut[l], preferred_element_type=jnp.float32)
+                e_t[l, subl, :] = (e_t[l + 1, subl, :].astype(jnp.float32) + back).astype(jnp.bfloat16)
+
+                @pl.when(l == 0)
+                def _():
+                    hop_down(p).start()
         return carry
 
     lax.fori_loop(0, n_layers, bwd_layer, 0)
-
-    @pl.when(not_first)
-    def _():
-        hop_down().start()
 
     for l in range(top):
         keep_e(l).start()
@@ -206,7 +255,7 @@
     def _():
         loss_down().wait_recv()
 
-    @pl.when(jnp.logical_not(not_last))
+    @pl.when(is_last)
     def _():
         for k in range(1, 2 * CHIPS):
             share_loss(k).wait_send()
@@ -234,7 +283,8 @@
 
     @pl.when(not_first)
     def _():
-        hop_down().wait_send()
+        hop_down(0).wait_send()
+        hop_down(1).wait_send()
         loss_down().wait_send()
 
 
@@ -267,12 +317,13 @@
             pltpu.SemaphoreType.DMA((3,)),
             pltpu.SemaphoreType.DMA((4,)),
             pltpu.SemaphoreType.DMA((8,)),
-            pltpu.SemaphoreType.DMA((3,)),
-            pltpu.SemaphoreType.DMA((3,)),
+            pltpu.SemaphoreType.DMA((3, 2)),
+            pltpu.SemaphoreType.DMA((3, 2)),
             pltpu.SemaphoreType.DMA((4, 3)),
             pltpu.SemaphoreType.DMA((4, 3)),
             pltpu.SemaphoreType.DMA((7,)),
             pltpu.SemaphoreType.DMA((7,)),
+            pltpu.SemaphoreType.REGULAR,
         ],
         compiler_params=pltpu.CompilerParams(collective_id=0, has_side_effects=True, vmem_limit_bytes=67043328),
     )(x_rows, y_rows, w_up, w_down)
@@ -311,7 +362,7 @@
     load_h(top).start()
     top_copy = pltpu.make_async_copy(e_top, e_buf.at[top], e_sem.at[top])
     top_copy.start()
-    for q in range(RING - 1):
+    for q in range(2):
         for cp in load_w(q):
             cp.start()
 
@@ -339,46 +390,40 @@
         keep(l).start()
         load_h(l).start()
 
-    def swap(l, par, k):
-        return pltpu.make_async_remote_copy(
-            src_ref=part.at[par, k, 1 - core], dst_ref=recv.at[l, k], send_sem=x_send.at[l, k], recv_sem=x_recv.at[l, k],
+    half_chunks = n_chunks // 2 + 1
+    groups = (slice(0, half_chunks * CHUNK), slice(half_chunks * CHUNK, ffn))
+
+    def swap(l, k, p):
+        return pltpu.make_async_remote_copy(
+            src_ref=part.at[l, k, 1 - core, :, groups[p]], dst_ref=recv.at[l, k, :, groups[p]],
+            send_sem=x_send.at[l, k, p], recv_sem=x_recv.at[l, k, p],
             device_id=(stage, partner), device_id_type=MESH)
 
-    def put_one(l, par):
-        return pltpu.make_async_copy(part.at[par, 0, core], out1.at[l], o_sem.at[0])
-
-    def put_two(l):
-        return pltpu.make_async_copy(turn, out2.at[l], o_sem.at[1])
-
-    def finish(l, par):
+    def put(l):
+        return (pltpu.make_async_copy(part.at[l, 0, core], out1.at[l], o_sem.at[0, l]),
+                pltpu.make_async_copy(turn.at[l % 2], out2.at[l], o_sem.at[1, l]))
+
+    def finish(l, c):
+        cols = pl.ds(pl.multiple_of(c * CHUNK, CHUNK), CHUNK)
+        part[l, 0, core, :, cols] = part[l, 0, core, :, cols] + recv[l, 0, :, cols]
+        both = part[l, 1, core, :, cols] + recv[l, 1, :, cols]
+        turn[l % 2, cols, :] = both.T
+
+    def swap_start(l, p):
         for k in range(2):
-            swap(l, par, k).wait_send()
-            swap(l, par, k).wait_recv()
-
-        def add(c, carry):
-            cols = pl.ds(pl.multiple_of(c * CHUNK, CHUNK), CHUNK)
-            part[par, 0, core, :, cols] = part[par, 0, core, :, cols] + recv[l, 0, :, cols]
-            both = part[par, 1, core, :, cols] + recv[l, 1, :, cols]
-            turn[cols, :] = both.T
-            return carry
-
-        lax.fori_loop(0, n_chunks, add, 0)
-        put_one(l, par).start()
-        put_two(l).start()
-        put_one(l, par).wait()
-        put_two(l).wait()
-
-    def layer_step(li, carry):
+            swap(l, k, p).start()
+
+    def swap_wait(l, p):
+        for k in range(2):
+            swap(l, k, p).wait_send()
+            swap(l, k, p).wait_recv()
+
+    def layer_step(li, first):
         l = top - li
-        par = li % 2
         load_h(l).wait()
-
-        @pl.when(li == 0)
-        def _():
+        if first:
             top_copy.wait()
-
-        @pl.when(li > 0)
-        def _():
+        else:
             keep(l).wait()
             for j in range(CHIPS - 1):
                 gather(l, j).wait_recv()
@@ -394,10 +439,6 @@
 
         def mm(c, u_ref, dg_ref):
             q = li * n_chunks + c
-            for cp in load_w(q):
-                cp.wait()
-            for cp in load_w(q + RING - 1):
-                cp.start()
             s = q % RING
             h = h_buf[l].reshape(n_rows, width)
             e = e_buf[l].reshape(n_rows, width)
@@ -415,31 +456,66 @@
             d1 = jnp.dot(hct[...], du, preferred_element_type=jnp.float32)
             d2 = jnp.dot(ect[...], g, preferred_element_type=jnp.float32)
             for k in range(2):
-                part[par, 0, k, :, cols] = d1[k * blk:(k + 1) * blk]
-                part[par, 1, k, :, cols] = d2[k * blk:(k + 1) * blk]
-
-        mm(0, u_a, dg_a)
+                part[l, 0, k, :, cols] = d1[k * blk:(k + 1) * blk]
+                part[l, 1, k, :, cols] = d2[k * blk:(k + 1) * blk]
+            if not first:
+                finish(l + 1, c)
 
         def pair(i, c2):
+            for n in (1, 2):
+                for cp in load_w(li * n_chunks + 2 * i + n):
+                    cp.wait()
+            for n in (3, 4):
+                for cp in load_w(li * n_chunks + 2 * i + n):
+                    cp.start()
             mm(2 * i + 1, u_b, dg_b)
             ew(2 * i, u_a, dg_a)
             mm(2 * i + 2, u_a, dg_a)
             ew(2 * i + 1, u_b, dg_b)
             return c2
 
-        lax.fori_loop(0, n_chunks // 2, pair, 0)
+        if not first:
+            swap_wait(l + 1, 0)
+        for cp in load_w(li * n_chunks):
+            cp.wait()
+        for cp in load_w(li * n_chunks + 2):
+            cp.start()
+        mm(0, u_a, dg_a)
+        lax.fori_loop(0, half_chunks // 2, pair, 0)
+        swap_start(l, 0)
+        if not first:
+            swap_wait(l + 1, 1)
+        lax.fori_loop(half_chunks // 2, n_chunks // 2, pair, 0)
         ew(n_chunks - 1, u_a, dg_a)
-        for k in range(2):
-            swap(l, par, k).start()
-
-        @pl.when(li > 0)
-        def _():
-            finish(l + 1, (li + 1) % 2)
+        swap_start(l, 1)
+        if not first:
+            for cp in put(l + 1):
+                cp.start()
+
+    layer_step(0, True)
+
+    def later(li, carry):
+        layer_step(li, False)
         return carry
 
-    lax.fori_loop(0, n_layers, layer_step, 0)
-    finish(0, top % 2)
-    for q in range(total, total + RING - 1):
+    lax.fori_loop(1, n_layers, later, 0)
+
+    def tail(c, carry):
+        finish(0, c)
+        return carry
+
+    for cp in put(2):
+        cp.wait()
+    swap_wait(0, 0)
+    lax.fori_loop(0, half_chunks, tail, 0)
+    swap_wait(0, 1)
+    lax.fori_loop(half_chunks, n_chunks, tail, 0)
+    for cp in put(0):
+        cp.start()
+    for l in (1, 0):
+        for cp in put(l):
+            cp.wait()
+    for q in range(total, total + 2):
         for cp in load_w(q):
             cp.wait()
     for l in range(top):
@@ -473,11 +549,11 @@
             pltpu.VMEM((CHIPS * rows, CHUNK), bf),
             pltpu.VMEM((CHIPS * rows, CHUNK), bf),
             pltpu.VMEM((CHIPS * rows, CHUNK), bf),
-            pltpu.VMEM((2, 2, 2, blk, ffn), f32),
+            pltpu.VMEM((n_layers, 2, 2, blk, ffn), f32),
             pltpu.VMEM((n_layers, 2, blk, ffn), f32),
-            pltpu.VMEM((ffn, blk), f32),
-            dma((2, RING)), dma((3,)), dma((3,)), dma((2,)),
-            dma((2, 3)), dma((2, 3)), dma((3, 2)), dma((3, 2)),
+            pltpu.VMEM((2, ffn, blk), f32),
+            dma((2, RING)), dma((3,)), dma((3,)), dma((2, 3)),
+            dma((2, 3)), dma((2, 3)), dma((3, 2, 2)), dma((3, 2, 2)),
         ],
         compiler_params=pltpu.CompilerParams(collective_id=1, has_side_effects=True, vmem_limit_bytes=67043328),
     )(h_gath, e_own, e_top, w_up, w_down)

time: 372 us -> 351 us (0.944)
  Pallas kernels: 355 us -> 335 us
    pallas_call x1, Pallas kernels: 124 us -> 111 us  [run_weights(): pl.pallas_call(weight_kernel, out_shape=(jax.ShapeDtypeStruct((n_layers,...]
    pallas_call x1, Pallas kernels: 230 us -> 223 us  [run_chain(): pl.pallas_call(functools.partial(chain_kernel, stages, total_tokens), out...]
where the time goes in v4:
time: 351 us
  Pallas kernels  335 us (95%)
  local copies, waits for them, and re-layouts  15.6 us (4%)
    pallas_call x1, Pallas kernels, run_chain(): pl.pallas_call(functools.partial(chain_kernel, stages, total_tokens), out...  223 us
    pallas_call x1, Pallas kernels, run_weights(): pl.pallas_call(weight_kernel, out_shape=(jax.ShapeDtypeStruct((n_layers,...  111 us
    unnamed x2, local copies, waits for them, and re-layouts  14.4 us

profile of v4, /device:TPU:0, one launch (start us, length us, event | category | flops | bytes accessed | tf_op | source)
XLA Modules:
  0.0 350.8 jit_solution(15447122448716994440)
XLA Ops:
  0.6 223.0 %shard_map.67 = (bf16[3,4,256,896]{3,2,1,0:T(8,128)(2,1)}, bf16[2,256,896]{2,1,0:T(8,128)(2,1)}, bf16[4,256,896]{2,1,0:T(8,128)(2,1)}, f32[8,128]{1,0:T(8,128)}) custom-call(bf16[256,896]{1,0:T(8,128)(2,1)} %bitcast.3, bf16[256,896]{1,0:T(8,128)(2,1)} %bitcast.4, bf16[3,896,4864]{2,1,0:T(8,128)(2,1)} %w1_hbm.3, bf16[3,4864,896]{2,1,0:T(8,128)(2,1)} %w2_hbm.3), custom_call_target="tpu_custom_call" | custom-call | tf_op jit(solution)/shard_map/pallas_call | solution.py:296
  223.7 1.2 slice.3
  224.9 111.5 %shard_map.68 = (f32[3,112,4864]{2,1,0:T(8,128)}, f32[3,4864,112]{2,1,0:T(8,128)}) custom-call(bf16[3,4,256,896]{3,2,1,0:T(8,128)(2,1)} %get-tuple-element.10.h_hbm, bf16[2,256,896]{2,1,0:T(8,128)(2,1)} %get-tuple-element.11.e_own, bf16[4,256,896]{2,1,0:T(8,128)(2,1)} %get-tuple-element.12.e_top, bf16[3,896,4864]{2,1,0:T(8,128)(2,1)} %w1_hbm.3, ...), custom_call_target="tpu_custom_call" | custom-call | tf_op jit(solution)/shard_map/pallas_call | solution.py:533
  336.4 8.4 %copy.7 = f32[3,4864,112]{1,2,0:T(8,128)} copy(f32[3,4864,112]{2,1,0:T(8,128)} %get-tuple-element.17) | data formatting | bytes 13074432
  344.7 6.1 %copy.9 = f32[3,112,4864]{2,1,0:T(8,128)} copy(f32[3,112,4864]{2,1,0:T(8,128)} %get-tuple-element.22) | data formatting | bytes 13074432

commit v5 on v4

--- a/solution.py
+++ b/solution.py
@@ -21,9 +21,8 @@
 
 def gelu_slope(u):
     sq = u * u
-    th = jnp.tanh(u * (GELU_C + (GELU_C * GELU_A) * sq))
-    half = 0.5 + 0.5 * th
-    return half + (0.5 * u) * (1.0 - th * th) * (GELU_C + (3.0 * GELU_C * GELU_A) * sq)
+    half = 0.5 + 0.5 * jnp.tanh(u * (GELU_C + (GELU_C * GELU_A) * sq))
+    return half + (half - half * half) * (u * (2.0 * GELU_C + (6.0 * GELU_C * GELU_A) * sq))
 
 
 def chain_kernel(stages, total_tokens, x_ref, y_ref, w1_hbm, w2_hbm, h_all, e_out, e_top, loss_ref,
@@ -132,6 +131,10 @@
         hop_up(0).wait_recv()
         hop_up(1).wait_recv()
 
+    @pl.when(jnp.logical_and(stage == 1, core == 0))
+    def _():
+        pl.semaphore_signal(turn_sem, inc=1, device_id=(stage - 1, data), device_id_type=MESH)
+
     @pl.when(is_first)
     def _():
         x_copy.wait()
@@ -191,6 +194,7 @@
 
     @pl.when(jnp.logical_and(is_first, core == 0))
     def _():
+        pl.semaphore_wait(turn_sem, 1)
         pl.semaphore_signal(turn_sem, inc=1, device_id=(stage, data + 1), device_id_type=MESH)
 
     @pl.when(not_last)
@@ -334,7 +338,7 @@
 
 
 def weight_kernel(h_hbm, e_own, e_top, w1_hbm, w2_hbm, out1, out2,
-                  h_buf, e_buf, w1s, w2s, hct, ect, u_a, dg_a, u_b, dg_b, part, recv, turn,
+                  h_buf, e_buf, w1s, w2s, hct, ect, u_a, dg_a, u_b, dg_b, part, recv,
                   w_sem, h_sem, e_sem, o_sem, ag_send, ag_recv, x_send, x_recv):
     stage = lax.axis_index('stage')
     data = lax.axis_index('data')
@@ -401,13 +405,12 @@
 
     def put(l):
         return (pltpu.make_async_copy(part.at[l, 0, core], out1.at[l], o_sem.at[0, l]),
-                pltpu.make_async_copy(turn.at[l % 2], out2.at[l], o_sem.at[1, l]))
+                pltpu.make_async_copy(part.at[l, 1, core], out2.at[l], o_sem.at[1, l]))
 
     def finish(l, c):
         cols = pl.ds(pl.multiple_of(c * CHUNK, CHUNK), CHUNK)
-        part[l, 0, core, :, cols] = part[l, 0, core, :, cols] + recv[l, 0, :, cols]
-        both = part[l, 1, core, :, cols] + recv[l, 1, :, cols]
-        turn[l % 2, cols, :] = both.T
+        for k in range(2):
+            part[l, k, core, :, cols] = part[l, k, core, :, cols] + recv[l, k, :, cols]
 
     def swap_start(l, p):
         for k in range(2):
@@ -534,7 +537,7 @@
         weight_kernel,
         out_shape=(
             jax.ShapeDtypeStruct((n_layers, blk, ffn), f32),
-            jax.ShapeDtypeStruct((n_layers, ffn, blk), f32),
+            jax.ShapeDtypeStruct((n_layers, blk, ffn), f32),
         ),
         in_specs=[any_spec] * 5,
         out_specs=(any_spec, any_spec),
@@ -551,12 +554,43 @@
             pltpu.VMEM((CHIPS * rows, CHUNK), bf),
             pltpu.VMEM((n_layers, 2, 2, blk, ffn), f32),
             pltpu.VMEM((n_layers, 2, blk, ffn), f32),
-            pltpu.VMEM((2, ffn, blk), f32),
             dma((2, RING)), dma((3,)), dma((3,)), dma((2, 3)),
             dma((2, 3)), dma((2, 3)), dma((3, 2, 2)), dma((3, 2, 2)),
         ],
         compiler_params=pltpu.CompilerParams(collective_id=1, has_side_effects=True, vmem_limit_bytes=67043328),
     )(h_gath, e_own, e_top, w_up, w_down)
+
+
+def place_kernel(a_hbm, b_hbm, a_out, b_out, a_buf, b_buf, sems):
+    n_layers = a_hbm.shape[0]
+    ins, outs = [], []
+    for l in range(n_layers):
+        for k, (src, buf, dst) in enumerate(((a_hbm, a_buf, a_out), (b_hbm, b_buf, b_out))):
+            ins.append(pltpu.make_async_copy(src.at[l], buf.at[l], sems.at[0, k, l]))
+            outs.append(pltpu.make_async_copy(buf.at[l], dst.at[l], sems.at[1, k, l]))
+    for cp in ins:
+        cp.start()
+    for cp_in, cp_out in zip(ins, outs):
+        cp_in.wait()
+        cp_out.start()
+    for cp in outs:
+        cp.wait()
+
+
+def place(grad_up, grad_down):
+    any_spec = pl.BlockSpec(memory_space=pl.ANY)
+    return pl.pallas_call(
+        place_kernel,
+        out_shape=tuple(jax.ShapeDtypeStruct(g.shape, g.dtype) for g in (grad_up, grad_down)),
+        in_specs=[any_spec] * 2,
+        out_specs=(any_spec, any_spec),
+        scratch_shapes=[
+            pltpu.VMEM(grad_up.shape, grad_up.dtype),
+            pltpu.VMEM(grad_down.shape, grad_down.dtype),
+            pltpu.SemaphoreType.DMA((2, 2, grad_up.shape[0])),
+        ],
+        compiler_params=pltpu.CompilerParams(vmem_limit_bytes=67043328),
+    )(grad_up, grad_down)
 
 
 def solution(mesh):
@@ -572,7 +606,8 @@
         y_rows = y_loc.reshape(rows, n_width)
         h_gath, e_own, e_top, loss = run_chain(x_rows, y_rows, w_up, w_down, stages, total_tokens)
         grad_up, grad_down = run_weights(h_gath, e_own, e_top, w_up, w_down)
-        return loss[0, 0], grad_up, grad_down
+        grad_up, grad_down = place(grad_up, grad_down)
+        return loss[0, 0], grad_up, jnp.swapaxes(grad_down, 1, 2)
 
     return jax.shard_map(
         per_device,

time: 351 us -> 341 us (0.972)
  local copies, waits for them, and re-layouts: 15.6 us -> 1.19 us
  Pallas kernels: 335 us -> 339 us
    unnamed x2 -> x0, local copies, waits for them, and re-layouts: 14.4 us -> none
    pallas_call x0 -> x1, Pallas kernels: none -> 9.16 us  [place(): pl.pallas_call(place_kernel, out_shape=tuple((jax.ShapeDtypeStruct(g.shap...]
    pallas_call x1, Pallas kernels: 223 us -> 218 us  [run_chain(): pl.pallas_call(functools.partial(chain_kernel, stages, total_tokens), out...]
where the time goes in v5:
time: 341 us
  Pallas kernels  339 us (99%)
    pallas_call x1, Pallas kernels, run_chain(): pl.pallas_call(functools.partial(chain_kernel, stages, total_tokens), out...  218 us
    pallas_call x1, Pallas kernels, run_weights(): pl.pallas_call(weight_kernel, out_shape=(jax.ShapeDtypeStruct((n_layers,...  112 us
    pallas_call x1, Pallas kernels, place(): pl.pallas_call(place_kernel, out_shape=tuple((jax.ShapeDtypeStruct(g.shap...  9.16 us

profile of v5, /device:TPU:0, one launch (start us, length us, event | category | flops | bytes accessed | tf_op | source)
XLA Modules:
  0.0 340.9 jit_solution(13407976739728013045)
XLA Ops:
  0.6 217.6 %shard_map.67 = (bf16[3,4,256,896]{3,2,1,0:T(8,128)(2,1)}, bf16[2,256,896]{2,1,0:T(8,128)(2,1)}, bf16[4,256,896]{2,1,0:T(8,128)(2,1)}, f32[8,128]{1,0:T(8,128)}) custom-call(bf16[256,896]{1,0:T(8,128)(2,1)} %bitcast.4, bf16[256,896]{1,0:T(8,128)(2,1)} %bitcast.5, bf16[3,896,4864]{2,1,0:T(8,128)(2,1)} %w1_hbm.3, bf16[3,4864,896]{2,1,0:T(8,128)(2,1)} %w2_hbm.3), custom_call_target="tpu_custom_call" | custom-call | tf_op jit(solution)/shard_map/pallas_call | solution.py:300
  218.2 1.2 slice.3
  219.4 112.2 %shard_map.68 = (f32[3,112,4864]{2,1,0:T(8,128)}, f32[3,112,4864]{2,1,0:T(8,128)}) custom-call(bf16[3,4,256,896]{3,2,1,0:T(8,128)(2,1)} %get-tuple-element.12.h_hbm, bf16[2,256,896]{2,1,0:T(8,128)(2,1)} %get-tuple-element.13.e_own, bf16[4,256,896]{2,1,0:T(8,128)(2,1)} %get-tuple-element.14.e_top, bf16[3,896,4864]{2,1,0:T(8,128)(2,1)} %w1_hbm.3, ...), custom_call_target="tpu_custom_call" | custom-call | tf_op jit(solution)/shard_map/pallas_call | solution.py:536
  331.6 9.2 %shard_map.69 = (f32[3,112,4864]{2,1,0:T(8,128)}, f32[3,112,4864]{2,1,0:T(8,128)}) custom-call(f32[3,112,4864]{2,1,0:T(8,128)} %get-tuple-element.15.a_hbm, f32[3,112,4864]{2,1,0:T(8,128)} %get-tuple-element.16.b_hbm), custom_call_target="tpu_custom_call" | custom-call | tf_op jit(solution)/shard_map/pallas_call | solution.py:582
